TPU v7x, 256 devices: a whole 4x4x8 slice. The times are simulated.
256 devices in a mesh: row: 16 (over x, y), col: 16 (over z, core).
Axes of the slice: x: 4, y: 4, z: 8, core: 2. Of those that a mesh axis runs over, the one named last changes fastest.
Arguments:
- loads: float32 [16, 16, 1024, 8], P('row', 'col'), may hold values from -6 to 6
- schur: float32 [16, 16, 1024, 1024], P('row', 'col'), may hold values from -0.5 to 4.5, as said below
- factor: float32 [16, 16, 1024, 1024], P('row', 'col'), may hold values from -0.5 to 0.6, as said below
- coarse_inverse: float32 [12288, 12288], P(('row', 'col')), may hold values from -0.5 to 1.5, as said below
- elements: int32 [16, 16], P('row', 'col'), may hold values from 4096 to 16383
- west_map: int32 [16, 16, 256], P('row', 'col'), may hold values from 0 to 255, each once within a row
- south_map: int32 [16, 16, 256], P('row', 'col'), may hold values from 0 to 255, each once within a row
- prim_local: int32 [16, 16, 48], P('row', 'col'), may hold values from 0 to 1023
- prim_coarse: int32 [16, 16, 48], P('row', 'col'), may hold values from 0 to 12287
Outputs:
- solution: float32 [16, 16, 1024, 8], P('row', 'col')
- residual: float32 [16, 16, 1024, 8], P('row', 'col')
Inputs may be any that keep to these rules, and one draw needn't show every extreme that they name: `schur`: symmetric positive definite. `factor`: symmetric positive definite. `coarse_inverse`: symmetric positive definite. `west_map`: each subdomain's row is a permutation of 0 to 255. `south_map`: each subdomain's row is a permutation of 0 to 255. `prim_local`: values may repeat. `prim_coarse`: values may repeat, within a subdomain and between subdomains.
All inputs are finite; a program needn't handle non-finite values.
Results may differ from a plain program's by a relative error of at most 0.0001.
Values sent between devices are 32-bit elements; how exact they have to be, the bound alone decides.
No kernel may reach another device: no remote copies, remote signals or barrier semaphores. Data moves between devices by JAX's collectives and lax.ppermute only.
A program may use at most 128 MiB of HBM per device.

v0:
```python
import jax
import jax.numpy as jnp
from jax import lax
from jax.sharding import Mesh
from jax.sharding import PartitionSpec as P

ELEM_BASE = 4096
COL = ("col_0", "col_1")
ROW = ("row_0", "row_1")
ROW_COL = ("row_0", "row_1", "col_0", "col_1")


HIGHEST_PRECISION = lax.Precision.HIGHEST


def from_behind(x, axis, by):
    devices = lax.axis_size(axis)
    pairs = [(i, i + by) for i in range(devices) if 0 <= i + by < devices]
    return lax.ppermute(x, axis, pairs)


def from_everyone(x, axis):
    copies = jnp.broadcast_to(x, (lax.axis_size(axis), *x.shape))
    return lax.all_to_all(copies, axis, split_axis=0, concat_axis=0, tiled=True)


def laid_out(tiles, dim):
    tiles = jnp.moveaxis(tiles, 0, dim)
    dims = tiles.shape
    return tiles.reshape(*dims[:dim], dims[dim] * dims[dim + 1], *dims[dim + 2 :])


def whole_of(x, axes, dim):
    far, near = axes
    first = from_everyone(x, far)
    tiles = jnp.swapaxes(from_everyone(first, near), 0, 1)
    return laid_out(tiles.reshape(-1, *x.shape), dim)


def taken_together(x, axis):
    return from_everyone(x, axis).sum(axis=0)


def over_axes(x, axes):
    far, near = axes
    return taken_together(taken_together(x, near), far)


def packed_total(arrays, axis):
    line, at, gathered = (jnp.concatenate([a.reshape(-1) for a in arrays]), 0, [])
    subtotal = over_axes(line, axis)
    for a in arrays:
        gathered.append(subtotal[at : at + a.size].reshape(a.shape))
        at += a.size
    return tuple(gathered)


def product(matrix, vectors):
    return jnp.dot(matrix, vectors, precision=HIGHEST_PRECISION, preferred_element_type=jnp.float32)


def body(
    loads, schur, factor, coarse_inverse, elements, west_map, south_map, prim_local, prim_coarse
):
    schur_block = schur[0, 0]
    factor_block = factor[0, 0]
    local_loads = loads[0, 0]
    sweep_count = elements[0, 0] // ELEM_BASE
    west_order = west_map[0, 0]
    south_order = south_map[0, 0]
    primal_local = prim_local[0, 0]
    primal_coarse = prim_coarse[0, 0]
    unknowns = schur_block.shape[0]
    face_size = unknowns // 4
    column = lax.axis_index(COL)
    grid_row = lax.axis_index(ROW)
    neighbour_flags = jnp.stack(
        [
            column > 0,
            column < lax.axis_size(COL) - 1,
            grid_row > 0,
            grid_row < lax.axis_size(ROW) - 1,
        ]
    )
    weights = jnp.where(neighbour_flags[jnp.arange(unknowns) // face_size], 0.5, 1.0).astype(
        jnp.float32
    )[:, None]

    def assemble(values):
        west_face = values[:face_size]
        east_face = values[face_size : 2 * face_size]
        south_face = values[2 * face_size : 3 * face_size]
        north_face = values[3 * face_size :]
        from_west = from_behind(east_face, COL, 1)
        west_add = jnp.take(from_west, west_order, axis=0)
        west_back = jnp.zeros_like(west_face).at[west_order].set(west_face)
        from_east = from_behind(west_back, COL, -1)
        from_south = from_behind(north_face, ROW, 1)
        south_add = jnp.take(from_south, south_order, axis=0)
        south_back = jnp.zeros_like(south_face).at[south_order].set(south_face)
        from_north = from_behind(south_back, ROW, -1)
        return values + jnp.concatenate([west_add, from_east, south_add, from_north], axis=0)

    def weighted_sum(first, second):
        return jnp.sum(weights * first * second, axis=0)

    all_primal = whole_of(primal_coarse, ("row_0", ("row_1", "col_0", "col_1")), 0)
    right_side = assemble(local_loads)
    residual = right_side
    scaled = weights * residual
    local = product(factor_block, scaled)

    def sweep(turn, present):
        return present + product(factor_block, scaled - product(schur_block, present))

    local = lax.fori_loop(1, sweep_count, sweep, local)
    picked = jnp.take(scaled, primal_local, axis=0)
    columns = jnp.take(coarse_inverse, all_primal, axis=1)
    solved = product(columns, whole_of(picked, ("row_0", ("row_1", "col_0", "col_1")), 0))
    whole = whole_of(solved, ("row_0", ("row_1", "col_0", "col_1")), 0)
    precond = assemble(
        weights
        * (
            local
            + jnp.zeros_like(scaled).at[primal_local].add(jnp.take(whole, primal_coarse, axis=0))
        )
    )
    image = assemble(product(schur_block, precond))
    gamma_now, delta_now = packed_total(
        (weighted_sum(residual, precond), weighted_sum(precond, image)),
        ("row_0", ("row_1", "col_0", "col_1")),
    )
    alpha = gamma_now / delta_now
    solution = alpha * precond
    residual = residual - alpha * image
    return (solution[None, None], residual[None, None])


def solution(mesh):
    torus = Mesh(mesh.devices.reshape(4, 4, 8, 2), ("row_0", "row_1", "col_0", "col_1"))
    return jax.shard_map(
        body,
        mesh=torus,
        in_specs=(
            P(ROW, COL, None, None),
            P(ROW, COL, None, None),
            P(ROW, COL, None, None),
            P(ROW_COL, None),
            P(ROW, COL),
            P(ROW, COL, None),
            P(ROW, COL, None),
            P(ROW, COL, None),
            P(ROW, COL, None),
        ),
        out_specs=(P(ROW, COL, None, None), P(ROW, COL, None, None)),
        check_vma=False,
    )
```

profile of v0, /device:TPU:1, one launch (start us, length us, event | category | flops | bytes accessed | tf_op | source)
XLA Modules:
  0.0 253.6 jit_solution(2926493052553794990)
XLA Ops:
  2.0 4.8 %all-to-all-start = ((s32[4,1,48]{2,1,0:T(1,128)}), s32[4,1,48]{2,1,0:T(1,128)S(1)}, u32[]{:S(2)}, u32[]{:S(2)}) async-start(s32[4,1,48]{2,1,0:T(1,128)} %broadcast_in_dim.90), calls=%async_computation | async-start | bytes 4096 | tf_op jit(solution)/shard_map/all_to_all | solution.py:24
  9.7 3.5 %collective-permute-start.1 = (f32[256,8]{0,1:T(8,128)S(1)}, f32[256,8]{0,1:T(8,128)S(1)}, u32[]{:S(2)}, u32[]{:S(2)}) collective-permute-start(f32[256,8]{0,1:T(8,128)S(1)} %copy.129), channel_id=1, source_target_pairs={{1,0},{2,1},{3,2},{4,3},{5,4},{6,5},{7,6},{8,7},{9,8},{10,9},{11,1... | collective-permute-start | bytes 24584 | tf_op jit(solution)/shard_map/ppermute | solution.py:19
  16.7 4.0 %collective-permute-start.2 = (f32[256,8]{1,0:T(8,128)S(1)}, f32[256,8]{1,0:T(8,128)S(1)}, u32[]{:S(2)}, u32[]{:S(2)}) collective-permute-start(f32[256,8]{1,0:T(8,128)S(1)} %bitcast.126), channel_id=1, source_target_pairs={{0,16},{16,32},{32,48},{48,64},{64,80},{80,96},{96,112},{112,128},... | collective-permute-start | bytes 24584 | tf_op jit(solution)/shard_map/ppermute | solution.py:19
  20.8 3.4 %collective-permute-start = (f32[256,8]{1,0:T(8,128)S(1)}, f32[256,8]{1,0:T(8,128)S(1)}, u32[]{:S(2)}, u32[]{:S(2)}) collective-permute-start(f32[256,8]{1,0:T(8,128)S(1)} %bitcast.125), channel_id=1, source_target_pairs={{0,1},{1,2},{2,3},{3,4},{4,5},{5,6},{6,7},{7,8},{8,9},{9,10},{10,1... | collective-permute-start | bytes 24584 | tf_op jit(solution)/shard_map/ppermute | solution.py:19
  33.7 5.5 %all-to-all-start.2 = ((f32[4,1,384]{2,1,0:T(1,128)}), f32[4,1,384]{2,1,0:T(1,128)S(1)}, u32[]{:S(2)}, u32[]{:S(2)}) async-start(f32[4,1,384]{2,1,0:T(1,128)} %reshape.446), calls=%async_computation.2 | async-start | bytes 12288 | tf_op jit(solution)/shard_map/all_to_all | solution.py:24
  39.9 4.0 %copy.136 = f32[48,12288]{0,1:T(8,128)} copy(f32[48,12288]{1,0:T(8,128)S(1)} %copy-done.1) | data formatting | bytes 4718592 | tf_op args[3]
  44.7 11.8 %all-to-all-start.1 = ((s32[64,1,192]{2,1,0:T(1,128)}), s32[64,1,192]{2,1,0:T(1,128)S(1)}, u32[]{:S(2)}, u32[]{:S(2)}) async-start(s32[64,1,192]{2,1,0:T(1,128)} %reshape.450), calls=%async_computation.1 | async-start | bytes 131072 | tf_op jit(solution)/shard_map/all_to_all | solution.py:24
  60.0 6.3 %all-to-all-done.1 = s32[64,1,192]{2,1,0:T(1,128)S(1)} async-done(((s32[64,1,192]{2,1,0:T(1,128)}), s32[64,1,192]{2,1,0:T(1,128)S(1)}, u32[]{:S(2)}, u32[]{:S(2)}) %all-to-all-start.1) | async-done | bytes 49184 | tf_op jit(solution)/shard_map/all_to_all | solution.py:24
  66.3 4.5 %all-to-all-start.3 = ((f32[64,1,1536]{2,1,0:T(1,128)}), f32[64,1,1536]{2,1,0:T(1,128)S(1)}, u32[]{:S(2)}, u32[]{:S(2)}) async-start(f32[64,1,1536]{2,1,0:T(1,128)} %reshape.448), calls=%async_computation.3 | async-start | bytes 786432 | tf_op jit(solution)/shard_map/all_to_all | solution.py:24
  72.6 43.8 %gather_fusion = f32[12288,48]{1,0:T(8,128)} fusion(f32[48,12288]{0,1:T(8,128)} %copy.136, s32[12288]{0:T(1024)S(1)} %broadcast_clamp_fusion), kind=kCustom, calls=%fused_computation.6 | custom fusion | bytes 4767744 | tf_op jit(solution)/shard_map/jit(_take)/gather | solution.py:118
  120.5 10.4 %fusion.1 = f32[48,8]{0,1:T(8,128)S(1)} fusion(f32[12288,8]{0,1:T(8,128)S(1)} %reshape_reshape.13, f32[12288,48]{1,0:T(8,128)} %gather_fusion, pred[12288]{0:T(1024)(128)(4,1)S(1)} %compare_and_fusion), kind=kOutput, calls=%fused_computation.19 | convolution fusion | flops 57212928 | bytes 2766336 | tf_op jit(solution)/shard_map/dot_general | solution.py:59
  131.6 4.2 %all-to-all-start.4 = ((f32[4,1,384]{2,1,0:T(1,128)}), f32[4,1,384]{2,1,0:T(1,128)S(1)}, u32[]{:S(2)}, u32[]{:S(2)}) async-start(f32[4,1,384]{2,1,0:T(1,128)} %reshape.452), calls=%async_computation.4 | async-start | bytes 12288 | tf_op jit(solution)/shard_map/all_to_all | solution.py:24
  135.8 5.7 %convolution_bitcast_fusion.2 = f32[1024,8]{0,1:T(8,128)S(1)} fusion(f32[1,1,1024,8]{2,3,1,0:T(8,128)S(1)} %copy-done.2, f32[1,1,256,8]{2,3,1,0:T(8,128)S(1)} %bitcast.128, f32[1,1,256,8]{2,3,1,0:T(8,128)S(1)} %bitcast.123, f32[1,1,256,8]{2,3,1,0:T(8,128)S(1)} %bitcast.127, f32[1,1,256,8]{2,3,1,0:T(8,128)S(1)} %bitcast.124, f32[1024]{0:T(1024)S(1)} %bitcast.119, ...), kind=kOutput, calls=%fused_computation.24 | convolution fusion | flops 100704256 | bytes 4296704 | tf_op jit(solution)/shard_map/dot_general | solution.py:59
  144.1 10.7 %all-to-all-start.5 = ((f32[64,1,1536]{2,1,0:T(1,128)}), f32[64,1,1536]{2,1,0:T(1,128)S(1)}, u32[]{:S(2)}, u32[]{:S(2)}) async-start(f32[64,1,1536]{2,1,0:T(1,128)} %reshape.454), calls=%async_computation.5 | async-start | bytes 786432 | tf_op jit(solution)/shard_map/all_to_all | solution.py:24
  154.8 9.7 %while.10 = (s32[]{:T(128)}, f32[1024,8]{0,1:T(8,128)S(1)}, s32[]{:T(128)}, f32[1024,1024]{1,0:T(8,128)}, f32[1024,8]{0,1:T(8,128)S(1)}, /*index=5*/f32[1024,1024]{1,0:T(8,128)}, s32[]{:T(128)}) while((s32[]{:T(128)}, f32[1024,8]{0,1:T(8,128)S(1)}, s32[]{:T(128)}, f32[1024,1024]{1,0:T(8,128)}, f32[1024,8]{0,1:T(8,128)S(1)}, ...), condition=%wide.region_3.5_spmd, body=%wide.region_2.4_spmd.sunk | while | flops 201342976 | bytes 25362536 | solution.py:116
  155.1 5.9 %convolution_subtract_fusion.2 = f32[1024,8]{0,1:T(8,128)S(1)} fusion(f32[1024,8]{0,1:T(8,128)S(1)} %get-tuple-element.123, f32[1024,1024]{1,0:T(8,128)} %get-tuple-element.122, f32[1024,8]{0,1:T(8,128)S(1)} %get-tuple-element.113), kind=kOutput, calls=%fused_computation.18.clone.1 | convolution fusion | flops 100671488 | bytes 4292608 | tf_op jit(solution)/shard_map/while/body/dot_general | solution.py:59
  161.0 3.6 %fusion.56 = f32[1024,8]{0,1:T(8,128)S(1)} fusion(f32[1024,8]{0,1:T(8,128)S(1)} %get-tuple-element.113, f32[1024,8]{0,1:T(8,128)S(1)} %convolution_subtract_fusion.2, f32[1024,1024]{1,0:T(8,128)S(1)} %copy-done), kind=kOutput, calls=%fused_computation.17.clone.1 | convolution fusion | flops 100671488 | bytes 4292608 | tf_op jit(solution)/shard_map/while/body/dot_general | solution.py:59
  164.7 4.6 %all-to-all-done.5 = f32[64,1,1536]{2,1,0:T(1,128)S(1)} async-done(((f32[64,1,1536]{2,1,0:T(1,128)}), f32[64,1,1536]{2,1,0:T(1,128)S(1)}, u32[]{:S(2)}, u32[]{:S(2)}) %all-to-all-start.5) | async-done | bytes 393248 | tf_op jit(solution)/shard_map/all_to_all | solution.py:24
  171.4 4.4 %copy.141 = f32[4,64,48,8]{3,2,1,0:T(8,128)} copy(f32[4,64,48,8]{2,3,0,1:T(8,128)S(1)} %bitcast_bitcast_fusion) | data formatting | bytes 786432 | tf_op jit(solution)/shard_map/transpose | solution.py:36
  188.0 6.4 %collective-permute-start.5 = (f32[256,8]{0,1:T(8,128)S(1)}, f32[256,8]{0,1:T(8,128)S(1)}, u32[]{:S(2)}, u32[]{:S(2)}) collective-permute-start(f32[256,8]{0,1:T(8,128)S(1)} %copy.147), channel_id=1, source_target_pairs={{1,0},{2,1},{3,2},{4,3},{5,4},{6,5},{7,6},{8,7},{9,8},{10,9},{11,1... | collective-permute-start | bytes 24584 | tf_op jit(solution)/shard_map/ppermute | solution.py:19
  196.3 5.6 %convolution_bitcast_fusion.1 = f32[1024,8]{0,1:T(8,128)S(1)} fusion(f32[1024,8]{0,1:T(8,128)S(1)} %maximum_add_fusion.2, f32[1,1,1024,1024]{3,2,1,0:T(8,128)} %bitcast.114), kind=kOutput, calls=%fused_computation.23 | convolution fusion | flops 100663296 | bytes 4259840 | tf_op jit(solution)/shard_map/dot_general | solution.py:59
  201.9 4.6 %collective-permute-start.10 = (f32[256,8]{0,1:T(8,128)S(1)}, f32[256,8]{0,1:T(8,128)S(1)}, u32[]{:S(2)}, u32[]{:S(2)}) collective-permute-start(f32[256,8]{0,1:T(8,128)S(1)} %get-tuple-element.53), channel_id=1, source_target_pairs={{0,16},{16,32},{32,48},{48,64},{64,80},{80,96},{96,112},{112,128},... | collective-permute-start | bytes 24584 | tf_op jit(solution)/shard_map/ppermute | solution.py:19
  219.0 23.3 %all_to_all.46 = f32[64,1,16]{2,1,0:T(1,128)S(1)} all-to-all(f32[64,1,16]{2,1,0:T(1,128)S(1)} %broadcast_in_dim.100), channel_id=1, replica_groups=mesh['row_0'=4,'row_1'=4,'col_0'=8,'col_1'=2] {'row_1','col_0','col_1'}, dimensions={0} | all-to-all | bytes 8192 | tf_op jit(solution)/shard_map/all_to_all | solution.py:24
  242.3 10.5 %all_to_all.47 = f32[4,1,16]{2,1,0:T(1,128)S(1)} all-to-all(f32[4,1,16]{2,1,0:T(1,128)S(1)} %broadcast_in_dim.101), channel_id=1, replica_groups=mesh['row_0'=4,'row_1'=4,'col_0'=8,'col_1'=2] {'row_0'}, dimensions={0} | all-to-all | bytes 512 | tf_op jit(solution)/shard_map/all_to_all | solution.py:24
  (140 shorter events, 60.0 us)
Async XLA Ops:
  0.6 39.2 %copy-start.1 = (f32[48,12288]{1,0:T(8,128)S(1)}, f32[48,12288]{1,0:T(8,128)}, u32[]{:S(2)}) copy-start(f32[48,12288]{1,0:T(8,128)} %param.16) | copy-start | bytes 7077892
  2.0 31.7 %all-to-all-start = ((s32[4,1,48]{2,1,0:T(1,128)}), s32[4,1,48]{2,1,0:T(1,128)S(1)}, u32[]{:S(2)}, u32[]{:S(2)}) async-start(s32[4,1,48]{2,1,0:T(1,128)} %broadcast_in_dim.90), calls=%async_computation | async-start | bytes 4096 | tf_op jit(solution)/shard_map/all_to_all | solution.py:24
  9.7 21.6 %collective-permute-start.1 = (f32[256,8]{0,1:T(8,128)S(1)}, f32[256,8]{0,1:T(8,128)S(1)}, u32[]{:S(2)}, u32[]{:S(2)}) collective-permute-start(f32[256,8]{0,1:T(8,128)S(1)} %copy.129), channel_id=1, source_target_pairs={{1,0},{2,1},{3,2},{4,3},{5,4},{6,5},{7,6},{8,7},{9,8},{10,9},{11,1... | collective-permute-start | bytes 24584 | tf_op jit(solution)/shard_map/ppermute | solution.py:19
  15.3 16.0 %collective-permute-start.3 = (f32[256,8]{0,1:T(8,128)S(1)}, f32[256,8]{0,1:T(8,128)S(1)}, u32[]{:S(2)}, u32[]{:S(2)}) collective-permute-start(f32[256,8]{0,1:T(8,128)S(1)} %copy.133), channel_id=1, source_target_pairs={{16,0},{32,16},{48,32},{64,48},{80,64},{96,80},{112,96},{128,112},... | collective-permute-start | bytes 24584 | tf_op jit(solution)/shard_map/ppermute | solution.py:19
  16.7 12.9 %collective-permute-start.2 = (f32[256,8]{1,0:T(8,128)S(1)}, f32[256,8]{1,0:T(8,128)S(1)}, u32[]{:S(2)}, u32[]{:S(2)}) collective-permute-start(f32[256,8]{1,0:T(8,128)S(1)} %bitcast.126), channel_id=1, source_target_pairs={{0,16},{16,32},{32,48},{48,64},{64,80},{80,96},{96,112},{112,128},... | collective-permute-start | bytes 24584 | tf_op jit(solution)/shard_map/ppermute | solution.py:19
  20.8 9.6 %collective-permute-start = (f32[256,8]{1,0:T(8,128)S(1)}, f32[256,8]{1,0:T(8,128)S(1)}, u32[]{:S(2)}, u32[]{:S(2)}) collective-permute-start(f32[256,8]{1,0:T(8,128)S(1)} %bitcast.125), channel_id=1, source_target_pairs={{0,1},{1,2},{2,3},{3,4},{4,5},{5,6},{6,7},{7,8},{8,9},{9,10},{10,1... | collective-permute-start | bytes 24584 | tf_op jit(solution)/shard_map/ppermute | solution.py:19
  33.7 11.0 %all-to-all-start.2 = ((f32[4,1,384]{2,1,0:T(1,128)}), f32[4,1,384]{2,1,0:T(1,128)S(1)}, u32[]{:S(2)}, u32[]{:S(2)}) async-start(f32[4,1,384]{2,1,0:T(1,128)} %reshape.446), calls=%async_computation.2 | async-start | bytes 12288 | tf_op jit(solution)/shard_map/all_to_all | solution.py:24
  44.7 21.6 %all-to-all-start.1 = ((s32[64,1,192]{2,1,0:T(1,128)}), s32[64,1,192]{2,1,0:T(1,128)S(1)}, u32[]{:S(2)}, u32[]{:S(2)}) async-start(s32[64,1,192]{2,1,0:T(1,128)} %reshape.450), calls=%async_computation.1 | async-start | bytes 131072 | tf_op jit(solution)/shard_map/all_to_all | solution.py:24
  66.3 50.1 %all-to-all-start.3 = ((f32[64,1,1536]{2,1,0:T(1,128)}), f32[64,1,1536]{2,1,0:T(1,128)S(1)}, u32[]{:S(2)}, u32[]{:S(2)}) async-start(f32[64,1,1536]{2,1,0:T(1,128)} %reshape.448), calls=%async_computation.3 | async-start | bytes 786432 | tf_op jit(solution)/shard_map/all_to_all | solution.py:24
  119.8 16.0 %copy-start.2 = (f32[1,1,1024,8]{2,3,1,0:T(8,128)S(1)}, f32[1,1,1024,8]{2,3,1,0:T(8,128)}, u32[]{:S(2)}) copy-start(f32[1,1,1024,8]{2,3,1,0:T(8,128)} %param.13) | copy-start | bytes 98308
  131.6 9.9 %all-to-all-start.4 = ((f32[4,1,384]{2,1,0:T(1,128)}), f32[4,1,384]{2,1,0:T(1,128)S(1)}, u32[]{:S(2)}, u32[]{:S(2)}) async-start(f32[4,1,384]{2,1,0:T(1,128)} %reshape.452), calls=%async_computation.4 | async-start | bytes 12288 | tf_op jit(solution)/shard_map/all_to_all | solution.py:24
  144.1 25.3 %all-to-all-start.5 = ((f32[64,1,1536]{2,1,0:T(1,128)}), f32[64,1,1536]{2,1,0:T(1,128)S(1)}, u32[]{:S(2)}, u32[]{:S(2)}) async-start(f32[64,1,1536]{2,1,0:T(1,128)} %reshape.454), calls=%async_computation.5 | async-start | bytes 786432 | tf_op jit(solution)/shard_map/all_to_all | solution.py:24
  155.0 5.9 %copy-start = (f32[1024,1024]{1,0:T(8,128)S(1)}, f32[1024,1024]{1,0:T(8,128)}, u32[]{:S(2)}) copy-start(f32[1024,1024]{1,0:T(8,128)} %get-tuple-element.124) | copy-start | bytes 12582916 | tf_op jit(solution)/shard_map/while
  178.0 16.4 %collective-permute-start.6 = (f32[256,8]{0,1:T(8,128)S(1)}, f32[256,8]{0,1:T(8,128)S(1)}, u32[]{:S(2)}, u32[]{:S(2)}) collective-permute-start(f32[256,8]{0,1:T(8,128)S(1)} %get-tuple-element.57), channel_id=1, source_target_pairs={{0,16},{16,32},{32,48},{48,64},{64,80},{80,96},{96,112},{112,128},... | collective-permute-start | bytes 24584 | tf_op jit(solution)/shard_map/ppermute | solution.py:19
  181.0 14.3 %collective-permute-start.4 = (f32[256,8]{0,1:T(8,128)S(1)}, f32[256,8]{0,1:T(8,128)S(1)}, u32[]{:S(2)}, u32[]{:S(2)}) collective-permute-start(f32[256,8]{0,1:T(8,128)S(1)} %get-tuple-element.55), channel_id=1, source_target_pairs={{0,1},{1,2},{2,3},{3,4},{4,5},{5,6},{6,7},{7,8},{8,9},{9,10},{10,1... | collective-permute-start | bytes 24584 | tf_op jit(solution)/shard_map/ppermute | solution.py:19
  185.3 10.9 %collective-permute-start.7 = (f32[256,8]{0,1:T(8,128)S(1)}, f32[256,8]{0,1:T(8,128)S(1)}, u32[]{:S(2)}, u32[]{:S(2)}) collective-permute-start(f32[256,8]{0,1:T(8,128)S(1)} %copy.151), channel_id=1, source_target_pairs={{16,0},{32,16},{48,32},{64,48},{80,64},{96,80},{112,96},{128,112},... | collective-permute-start | bytes 24584 | tf_op jit(solution)/shard_map/ppermute | solution.py:19
  188.0 8.3 %collective-permute-start.5 = (f32[256,8]{0,1:T(8,128)S(1)}, f32[256,8]{0,1:T(8,128)S(1)}, u32[]{:S(2)}, u32[]{:S(2)}) collective-permute-start(f32[256,8]{0,1:T(8,128)S(1)} %copy.147), channel_id=1, source_target_pairs={{1,0},{2,1},{3,2},{4,3},{5,4},{6,5},{7,6},{8,7},{9,8},{10,9},{11,1... | collective-permute-start | bytes 24584 | tf_op jit(solution)/shard_map/ppermute | solution.py:19
  201.9 13.7 %collective-permute-start.10 = (f32[256,8]{0,1:T(8,128)S(1)}, f32[256,8]{0,1:T(8,128)S(1)}, u32[]{:S(2)}, u32[]{:S(2)}) collective-permute-start(f32[256,8]{0,1:T(8,128)S(1)} %get-tuple-element.53), channel_id=1, source_target_pairs={{0,16},{16,32},{32,48},{48,64},{64,80},{80,96},{96,112},{112,128},... | collective-permute-start | bytes 24584 | tf_op jit(solution)/shard_map/ppermute | solution.py:19
  206.6 10.0 %collective-permute-start.8 = (f32[256,8]{0,1:T(8,128)S(1)}, f32[256,8]{0,1:T(8,128)S(1)}, u32[]{:S(2)}, u32[]{:S(2)}) collective-permute-start(f32[256,8]{0,1:T(8,128)S(1)} %get-tuple-element.51), channel_id=1, source_target_pairs={{0,1},{1,2},{2,3},{3,4},{4,5},{5,6},{6,7},{7,8},{8,9},{9,10},{10,1... | collective-permute-start | bytes 24584 | tf_op jit(solution)/shard_map/ppermute | solution.py:19
  211.0 6.5 %collective-permute-start.11 = (f32[256,8]{0,1:T(8,128)S(1)}, f32[256,8]{0,1:T(8,128)S(1)}, u32[]{:S(2)}, u32[]{:S(2)}) collective-permute-start(f32[256,8]{0,1:T(8,128)S(1)} %copy.159), channel_id=1, source_target_pairs={{16,0},{32,16},{48,32},{64,48},{80,64},{96,80},{112,96},{128,112},... | collective-permute-start | bytes 24584 | tf_op jit(solution)/shard_map/ppermute | solution.py:19
  213.7 5.0 %collective-permute-start.9 = (f32[256,8]{0,1:T(8,128)S(1)}, f32[256,8]{0,1:T(8,128)S(1)}, u32[]{:S(2)}, u32[]{:S(2)}) collective-permute-start(f32[256,8]{0,1:T(8,128)S(1)} %copy.155), channel_id=1, source_target_pairs={{1,0},{2,1},{3,2},{4,3},{5,4},{6,5},{7,6},{8,7},{9,8},{10,9},{11,1... | collective-permute-start | bytes 24584 | tf_op jit(solution)/shard_map/ppermute | solution.py:19
where the time goes:
time: 255 us; the launch traced here: 254 us
  local copies, waits for them, and re-layouts  80.2 us (31%)
  starting transfers between devices  78.2 us (31%)
  blocking collectives  33.7 us (13%)
  matrix products  31.1 us (12%)
  other arithmetic  16 us (6%)
  waiting for transfers between devices  12.1 us (5%)
    gather x1, local copies, waits for them, and re-layouts, body(): columns = jnp.take(coarse_inverse, all_primal, axis=1)  43.8 us
    all_to_all x6, starting transfers between devices, from_everyone(): return lax.all_to_all(copies, axis, split_axis=0, concat_axis=0, tiled=True)  41.6 us
    ppermute x12, starting transfers between devices, from_behind(): return lax.ppermute(x, axis, pairs)  36.7 us
    all_to_all x2, blocking collectives, from_everyone(): return lax.all_to_all(copies, axis, split_axis=0, concat_axis=0, tiled=True)  33.7 us
    dot_general x5, matrix products, product(): jnp.dot(matrix, vectors, precision=HIGHEST_PRECISION, preferred_element_t...  31.1 us
    unnamed x21, local copies, waits for them, and re-layouts  12.4 us
    all_to_all x6, waiting for transfers between devices, from_everyone(): return lax.all_to_all(copies, axis, split_axis=0, concat_axis=0, tiled=True)  10.9 us
    all_to_all x5, other arithmetic, from_everyone(): return lax.all_to_all(copies, axis, split_axis=0, concat_axis=0, tiled=True)  5.14 us
  transfers between devices with their start and end apart: 18, of which 3 were waited for; matrix products, arithmetic and copies ran while one was open for 37% of the time, Pallas kernels for 0%

commit v1 on v0

v1 whole, which is shorter than its diff:
```python
import jax
import jax.numpy as jnp
from jax import lax
from jax.experimental import pallas as pl
from jax.experimental.pallas import tpu as pltpu
from jax.sharding import PartitionSpec as P

ELEM_BASE = 4096
ROW, COL = "row", "col"
F32, BF16 = jnp.float32, jnp.bfloat16
VM = pl.BlockSpec(memory_space=pltpu.VMEM)
SM = pl.BlockSpec(memory_space=pltpu.SMEM)
LANES = 128
NPRIM = 48
SIDE = 16
IDX_AT = 64
RADIX = 256


def call(body, outs, specs, scratch=(), flops=0, moved=0):
    return pl.pallas_call(
        body,
        out_shape=outs,
        in_specs=specs,
        out_specs=jax.tree.map(lambda _: VM, outs),
        scratch_shapes=list(scratch),
        cost_estimate=pl.CostEstimate(flops=flops, transcendentals=0, bytes_accessed=moved),
        name=body.__name__,
    )


def shape(*dims, dtype=F32):
    return jax.ShapeDtypeStruct(dims, dtype)


def halves(x):
    high = x.astype(BF16)
    return high, (x - high.astype(F32)).astype(BF16)


def thirds(x):
    high = x.astype(BF16)
    rest = x - high.astype(F32)
    middle = rest.astype(BF16)
    low = (rest - middle.astype(F32)).astype(BF16)
    return high, middle, low


def nn(a, b):
    return lax.dot_general(a, b, (((1,), (0,)), ((), ())), preferred_element_type=F32)


def nt(a, b):
    return lax.dot_general(a, b, (((1,), (1,)), ((), ())), preferred_element_type=F32)


def one_hot(shape_, row):
    return jnp.where(lax.broadcasted_iota(jnp.int32, shape_, 0) == row, 1.0, 0.0).astype(BF16)


def selected(x, matrix, product):
    high, middle, low = thirds(x)
    return product(high, matrix) + product(middle, matrix) + product(low, matrix)


def times(x, high, low):
    x_high, x_low = halves(x)
    return nn(x_high, high) + nn(x_low, high) + nn(x_high, low)


def weight_row(row, col, unknowns):
    face = lax.broadcasted_iota(jnp.int32, (8, unknowns), 1) // (unknowns // 4)
    inner = jnp.where(face == 0, jnp.where(col > 0, 1, 0), jnp.where(col < SIDE - 1, 1, 0))
    outer = jnp.where(face == 2, jnp.where(row > 0, 1, 0), jnp.where(row < SIDE - 1, 1, 0))
    return jnp.where(jnp.where(face < 2, inner, outer) > 0, 0.5, 1.0).astype(F32)


def faces(x):
    size = x.shape[1] // 4
    return [x[:, i * size : (i + 1) * size] for i in range(4)]


def write_sends(values, orders, row, col, sends):
    west, east, south, north = faces(values)
    size = west.shape[1]
    for near, far, order, place, first, second in (
        (west, east, orders[0], col, sends[0], sends[1]),
        (south, north, orders[1], row, sends[2], sends[3]),
    ):
        back = selected(near, one_hot((size, size), order), nt)
        even = place % 2 == 0
        first[...] = jnp.where(even, far, back)
        second[...] = jnp.where(even, back, far)


def halo(got, orders, row, col):
    parts = []
    for order, place, first, second in (
        (orders[0], col, got[0], got[1]),
        (orders[1], row, got[2], got[3]),
    ):
        even = place % 2 == 0
        behind = jnp.where(even, second, first)
        ahead = jnp.where(even, first, second)
        size = behind.shape[1]
        picked = selected(behind, one_hot((size, size), order), nn)
        parts.append(jnp.where(place > 0, picked, 0.0))
        parts.append(jnp.where(place < SIDE - 1, ahead, 0.0))
    return jnp.concatenate(parts, axis=1)


def split_matrices(schur, factor, coarse, *outs):
    for k, ref in enumerate((schur, factor, coarse)):
        high, low = halves(ref[...])
        outs[2 * k][...] = high
        outs[2 * k + 1][...] = low


def first_sends(place, loads, west, south, *sends):
    write_sends(loads[...], (west[...], south[...]), place[0], place[1], sends)


def right_side(place, loads, g0, g1, g2, g3, west, south, local_at, coarse_at, b_ref, scaled_ref, slots):
    row, col = place[0], place[1]
    b = loads[...] + halo([g0[...], g1[...], g2[...], g3[...]], (west[...], south[...]), row, col)
    scaled = weight_row(row, col, b.shape[1]) * b
    b_ref[...] = b
    scaled_ref[...] = scaled
    picked = selected(scaled, one_hot((b.shape[1], LANES), local_at[...]), nn)
    lane = lax.broadcasted_iota(jnp.int32, (8, LANES), 1)
    tile = jnp.where(lane < NPRIM, picked, 0.0)
    index = jnp.broadcast_to(coarse_at[...].astype(F32), (8, LANES))
    index = pltpu.roll(index, IDX_AT, 1)
    tile = jnp.where((lane >= IDX_AT) & (lane < IDX_AT + NPRIM), index, tile)
    for i in range(SIDE):
        slots[i] = tile


def packed(tile_of, at):
    lane = lax.broadcasted_iota(jnp.int32, (8, LANES), 1)
    count = SIDE * NPRIM // LANES
    out = [jnp.zeros((8, LANES), F32) for _ in range(count)]
    for i in range(SIDE):
        start = i * NPRIM
        t, off = start // LANES, start % LANES
        moved = pltpu.roll(tile_of(i), (off - at) % LANES, 1)
        out[t] = jnp.where((lane >= off) & (lane < off + NPRIM), moved, out[t])
        if off + NPRIM > LANES:
            out[t + 1] = jnp.where(lane < off + NPRIM - LANES, moved, out[t + 1])
    return out


def pack_picked(got, coarse_at, slots):
    values = packed(lambda i: got[i], 0)
    index = packed(lambda i: got[i], IDX_AT)
    below = lax.broadcasted_iota(jnp.int32, (8, LANES), 0)
    last = jnp.broadcast_to(coarse_at[...].astype(F32), (8, LANES))
    for t, tile in enumerate(index):
        last = jnp.where(below == t, tile, last)
    for i in range(SIDE):
        for t, tile in enumerate(values + [last]):
            slots[i, :, t * LANES : (t + 1) * LANES] = tile


def coarse_solve(got, high, low, slots, spread, hot, total, rhs):
    width = SIDE * NPRIM
    blocks = high.shape[1] // RADIX
    total[...] = jnp.zeros_like(total)
    rows16 = lax.broadcasted_iota(jnp.int32, (16, LANES), 0).astype(F32)

    def group(step, carry):
        for part in range(2):
            g = step * 2 + part
            tiles = got[g]
            for t in range(width // LANES):
                value = tiles[:, t * LANES : (t + 1) * LANES]
                index = jnp.broadcast_to(tiles[t : t + 1, width : width + LANES], (16, LANES))
                block = jnp.floor(index * (1.0 / RADIX))
                within = (index - block * RADIX).astype(BF16)
                block = block.astype(BF16)
                v_high = value.astype(BF16).astype(F32)
                both = jnp.concatenate([v_high, value - v_high], axis=0).astype(BF16)
                at = part * width + t * LANES
                for l in range(blocks):
                    spread[16 * l : 16 * l + 16, at : at + LANES] = jnp.where(
                        block == jnp.asarray(l, BF16), both, jnp.zeros_like(both)
                    )
                for l in range(RADIX // 16):
                    hot[16 * l : 16 * l + 16, at : at + LANES] = jnp.where(
                        within == (rows16 + 16.0 * l).astype(BF16),
                        jnp.ones_like(both),
                        jnp.zeros_like(both),
                    )
        total[...] += nt(spread[...], hot[...])
        return carry

    lax.fori_loop(0, SIDE // 2, group, 0)
    for l in range(blocks):
        value = total[16 * l : 16 * l + 8] + total[16 * l + 8 : 16 * l + 16]
        v_high = value.astype(BF16).astype(F32)
        rhs[:, l * RADIX : (l + 1) * RADIX] = jnp.concatenate(
            [v_high, value - v_high], axis=0
        ).astype(BF16)
    first = nt(rhs[...], high[...])
    second = nt(rhs[...], low[...])
    solved = first[:8] + first[8:] + second[:8]
    tile = jnp.concatenate([solved, jnp.zeros((8, LANES - NPRIM), F32)], axis=1)
    for i in range(SIDE):
        slots[i] = tile


def pack_solved(place, got, asked, slots):
    width = SIDE * NPRIM
    mine = jnp.concatenate(packed(lambda i: got[i], 0), axis=1)
    parts = jnp.concatenate([p.astype(F32) for p in thirds(mine)], axis=0)
    parts = jnp.concatenate([parts, jnp.zeros((8, width), F32)], axis=0).astype(BF16)
    lane = lax.broadcasted_iota(jnp.int32, (1, LANES), 1)
    for i in range(SIDE):
        want = asked[i, width // LANES : width // LANES + 1, width : width + LANES]
        want = jnp.where(lane < NPRIM, want.astype(jnp.int32) - width * place[0], -1)
        found = nn(parts, one_hot((width, LANES), want))
        slots[i] = found[:8] + found[8:16] + found[16:24]


def corrected(place, got, local_at, local, b, west, south, t_ref, gamma, s0, s1, s2, s3):
    row, col = place[0], place[1]
    rows = got[0]
    for i in range(1, SIDE):
        rows = rows + got[i]
    unknowns = local.shape[1]
    lane = lax.broadcasted_iota(jnp.int32, (8, LANES), 1)
    rows = jnp.where(lane < NPRIM, rows, 0.0)
    correction = selected(rows, one_hot((unknowns, LANES), local_at[...]), nt)
    t = weight_row(row, col, unknowns) * (local[...] + correction)
    t_ref[...] = t
    gamma[...] = jnp.broadcast_to(jnp.sum(b[...] * t, axis=1, keepdims=True), (8, LANES))
    write_sends(t, (west[...], south[...]), row, col, (s0, s1, s2, s3))


def apply_operator(place, t, g0, g1, g2, g3, west, south, high, low, gamma, p_ref, u_ref, s0, s1, s2, s3, slots):
    row, col = place[0], place[1]
    orders = (west[...], south[...])
    p = t[...] + halo([g0[...], g1[...], g2[...], g3[...]], orders, row, col)
    u = times(p, high[...], low[...])
    p_ref[...] = p
    u_ref[...] = u
    write_sends(u, orders, row, col, (s0, s1, s2, s3))
    delta = jnp.broadcast_to(jnp.sum(p * u, axis=1, keepdims=True), (8, LANES))
    lane = lax.broadcasted_iota(jnp.int32, (8, LANES), 1)
    tile = jnp.where(lane == 0, gamma[...], delta)
    for i in range(SIDE):
        slots[i] = tile


def subtotal(got, slots):
    tile = got[0]
    for i in range(1, SIDE):
        tile = tile + got[i]
    for i in range(SIDE):
        slots[i] = tile


def finish(place, got, g0, g1, g2, g3, west, south, p, u, b, solution_ref, residual_ref):
    tile = got[0]
    for i in range(1, SIDE):
        tile = tile + got[i]
    alpha = tile[:, 0:1] / tile[:, 1:2]
    q = u[...] + halo([g0[...], g1[...], g2[...], g3[...]], (west[...], south[...]), place[0], place[1])
    solution_ref[...] = alpha * p[...]
    residual_ref[...] = b[...] - alpha * q


def first_solve(scaled, high, low, local):
    local[...] = times(scaled[...], high[...], low[...])


def sweep(turn):
    def sweep_once(elements, scaled, present, s_high, s_low, f_high, f_low, local):
        rest = scaled[...] - times(present[...], s_high[...], s_low[...])
        after = present[...] + times(rest, f_high[...], f_low[...])
        local[...] = jnp.where(elements[0, 0] // ELEM_BASE > turn, after, present[...])

    return sweep_once


def swapped(sends):
    even = [(i, i ^ 1) for i in range(SIDE)]
    odd = [(i, ((i + 1) ^ 1) - 1) for i in range(1, SIDE - 1)] + [(0, SIDE - 1), (SIDE - 1, 0)]
    return [
        lax.ppermute(x, axis, pairs)
        for x, axis, pairs in zip(sends, (COL, COL, ROW, ROW), (even, odd, even, odd))
    ]


def across(slots, axis):
    return lax.all_to_all(slots, axis, split_axis=0, concat_axis=0, tiled=True)


def body(
    loads, schur, factor, coarse_inverse, elements, west_map, south_map, prim_local, prim_coarse
):
    loads_t = loads[0, 0].T
    unknowns = loads_t.shape[1]
    face = unknowns // 4
    matrix = (unknowns, unknowns)
    place = jnp.stack([lax.axis_index(ROW), lax.axis_index(COL)]).astype(jnp.int32)
    west, south = west_map[0], south_map[0]
    pad = ((0, 0), (0, LANES - NPRIM))
    local_at = jnp.pad(prim_local[0], pad, constant_values=-1)
    coarse_at = jnp.pad(prim_coarse[0], pad)
    field = shape(8, unknowns)
    sends_shape = [shape(8, face)] * 4
    tiles = shape(SIDE, 8, LANES)
    width = SIDE * NPRIM
    product_flops = 2 * 1024 * unknowns * unknowns

    sends = call(first_sends, sends_shape, [SM] + [VM] * 3)(place, loads_t, west, south)
    s_high, s_low, f_high, f_low, c_high, c_low = call(
        split_matrices,
        [shape(*matrix, dtype=BF16)] * 4 + [shape(*coarse_inverse.shape, dtype=BF16)] * 2,
        [VM] * 3,
        flops=product_flops,
    )(schur[0, 0], factor[0, 0], coarse_inverse)
    got = swapped(sends)
    b, scaled, slots = call(right_side, [field, field, tiles], [SM] + [VM] * 9)(
        place, loads_t, *got, west, south, local_at, coarse_at
    )
    local = call(first_solve, field, [VM] * 3, flops=product_flops)(scaled, f_high, f_low)
    for turn in (1, 2):
        local = call(sweep(turn), field, [SM] + [VM] * 6, flops=2 * product_flops)(
            elements, scaled, local, s_high, s_low, f_high, f_low
        )
    gathered = across(slots, COL)
    slots = call(pack_picked, shape(SIDE, 8, width + LANES), [VM] * 2)(gathered, coarse_at)
    asked = across(slots, ROW)
    rows = 16 * coarse_inverse.shape[1] // RADIX
    slots = call(
        coarse_solve,
        tiles,
        [VM] * 3,
        scratch=(
            pltpu.VMEM((rows, 2 * width), BF16),
            pltpu.VMEM((RADIX, 2 * width), BF16),
            pltpu.VMEM((rows, RADIX), F32),
            pltpu.VMEM((16, coarse_inverse.shape[1]), BF16),
        ),
    )(asked, c_high, c_low)
    gathered = across(slots, COL)
    slots = call(pack_solved, tiles, [SM] + [VM] * 2)(place, gathered, asked)
    gathered = across(slots, ROW)
    t, gamma, *sends = call(corrected, [field, shape(8, LANES)] + sends_shape, [SM] + [VM] * 6)(
        place, gathered, local_at, local, b, west, south
    )
    got = swapped(sends)
    p, u, *rest = call(
        apply_operator, [field, field] + sends_shape + [tiles], [SM] + [VM] * 10
    )(place, t, *got, west, south, s_high, s_low, gamma)
    sends, slots = rest[:4], rest[4]
    got = swapped(sends)
    gathered = across(slots, COL)
    slots = call(subtotal, tiles, [VM])(gathered)
    gathered = across(slots, ROW)
    solution, residual = call(finish, [field, field], [SM] + [VM] * 10)(
        place, gathered, *got, west, south, p, u, b
    )
    return solution.T[None, None], residual.T[None, None]


def solution(mesh):
    return jax.shard_map(
        body,
        mesh=mesh,
        in_specs=(
            P(ROW, COL, None, None),
            P(ROW, COL, None, None),
            P(ROW, COL, None, None),
            P((ROW, COL), None),
            P(ROW, COL),
            P(ROW, COL, None),
            P(ROW, COL, None),
            P(ROW, COL, None),
            P(ROW, COL, None),
        ),
        out_specs=(P(ROW, COL, None, None), P(ROW, COL, None, None)),
        check_vma=False,
    )
```

time: 255 us -> 143 us (0.56)
  local copies, waits for them, and re-layouts: 80.2 us -> 6.77 us
  Pallas kernels: 0 us -> 52.1 us
  starting transfers between devices: 78.2 us -> 41.8 us
  matrix products: 31.1 us -> 0 us
  other arithmetic: 16 us -> 0.56 us
  waiting for transfers between devices: 12.1 us -> 8.35 us
    pallas_call x0 -> x13, Pallas kernels: none -> 52.1 us  [the longest x2 11.8 us: body(): call(sweep(turn), field, [SM] + [VM] * 6, flops=2 * product_flops)]
    gather x14 -> x0, local copies, waits for them, and re-layouts: 49.2 us -> none  [the longest x1 43.8 us: body(): columns = jnp.take(coarse_inverse, all_primal, axis=1)]
    dot_general x5 -> x0, matrix products: 31.1 us -> none  [product(): jnp.dot(matrix, vectors, precision=HIGHEST_PRECISION, preferred_element_t...]
    all_to_all x6 -> x4, starting transfers between devices: 41.6 us -> 20.8 us  [across(): return lax.all_to_all(slots, axis, split_axis=0, concat_axis=0, tiled=True)]
    ppermute x12, starting transfers between devices: 36.7 us -> 20.9 us  [swapped(): lax.ppermute(x, axis, pairs)]
    all_to_all x6 -> x4, waiting for transfers between devices: 10.9 us -> 2.53 us  [across(): return lax.all_to_all(slots, axis, split_axis=0, concat_axis=0, tiled=True)]
    unnamed x21 -> x32, local copies, waits for them, and re-layouts: 12.4 us -> 4.39 us
    scatter x12 -> x0, local copies, waits for them, and re-layouts: 7.48 us -> none  [the longest x6 3.74 us: assemble(): west_back = jnp.zeros_like(west_face).at[west_order].set(west_face)]
  transfers between devices with their start and end apart: 18 -> 16, of which waited for: 3 -> 5; matrix products, arithmetic and copies ran while one was open for 37% -> 2% of each run, Pallas kernels for 0% -> 17%
where the time goes in v1:
time: 143 us
  Pallas kernels  52.1 us (36%)
  starting transfers between devices  41.8 us (29%)
  blocking collectives  31.5 us (22%)
  waiting for transfers between devices  8.35 us (6%)
  local copies, waits for them, and re-layouts  6.77 us (5%)
    all_to_all x2, blocking collectives, across(): return lax.all_to_all(slots, axis, split_axis=0, concat_axis=0, tiled=True)  31.5 us
    ppermute x12, starting transfers between devices, swapped(): lax.ppermute(x, axis, pairs)  20.9 us
    all_to_all x4, starting transfers between devices, across(): return lax.all_to_all(slots, axis, split_axis=0, concat_axis=0, tiled=True)  20.8 us
    pallas_call x2, Pallas kernels, body(): call(sweep(turn), field, [SM] + [VM] * 6, flops=2 * product_flops)  11.8 us
    pallas_call x1, Pallas kernels, body(): call(coarse_solve, tiles, [VM] * 3, scratch=(pltpu.VMEM((rows, 2 * width)...  10.4 us
    pallas_call x1, Pallas kernels, body(): call(split_matrices, [shape(*matrix, dtype=BF16)] * 4 + [shape(*coarse_in...  8.59 us
    ppermute x12, waiting for transfers between devices, swapped(): lax.ppermute(x, axis, pairs)  5.82 us
    unnamed x32, local copies, waits for them, and re-layouts  4.39 us
  transfers between devices with their start and end apart: 16, of which 5 were waited for; matrix products, arithmetic and copies ran while one was open for 2% of the time, Pallas kernels for 17%

profile of v1, /device:TPU:1, one launch (start us, length us, event | category | flops | bytes accessed | tf_op | source)
XLA Modules:
  0.0 142.5 jit_solution(5956065994492600343)
XLA Ops:
  1.2 1.8 %first_sends.1 = (f32[8,256]{1,0:T(8,128)}, f32[8,256]{1,0:T(8,128)}, f32[8,256]{1,0:T(8,128)}, f32[8,256]{1,0:T(8,128)}) custom-call(s32[2]{0:T(128)} %pad_add_fusion.place, f32[8,1024]{1,0:T(8,128)} %bitcast.19, s32[1,256]{1,0:T(1,128)} %bitcast.21, s32[1,256]{1,0:T(1,128)} %bitcast.26), custom_call_target="tpu_custom_call" | custom-call | tf_op jit(solution)/shard_map/first_sends/pallas_call | solution.py:317
  3.0 3.2 %collective-permute-start = (f32[8,256]{1,0:T(8,128)}, f32[8,256]{1,0:T(8,128)S(1)}, u32[]{:S(2)}, u32[]{:S(2)}) collective-permute-start(f32[8,256]{1,0:T(8,128)} %get-tuple-element.30), channel_id=1, source_target_pairs={{0,1},{1,0},{2,3},{3,2},{4,5},{5,4},{6,7},{7,6},{8,9},{9,8},{10,11... | collective-permute-start | bytes 24584 | tf_op jit(solution)/shard_map/ppermute | solution.py:290
  7.4 4.1 %collective-permute-start.3 = (f32[8,256]{1,0:T(8,128)}, f32[8,256]{1,0:T(8,128)S(1)}, u32[]{:S(2)}, u32[]{:S(2)}) collective-permute-start(f32[8,256]{1,0:T(8,128)} %get-tuple-element.33), channel_id=1, source_target_pairs={{16,32},{32,16},{48,64},{64,48},{80,96},{96,80},{112,128},{128,112... | collective-permute-start | bytes 24584 | tf_op jit(solution)/shard_map/ppermute | solution.py:290
  15.1 1.9 %right_side.1 = (f32[8,1024]{1,0:T(8,128)}, f32[8,1024]{1,0:T(8,128)}, f32[16,8,128]{2,1,0:T(8,128)}) custom-call(s32[2]{0:T(128)} %pad_add_fusion.place, f32[8,1024]{1,0:T(8,128)} %bitcast.20, f32[8,256]{1,0:T(8,128)} %copy-done.10, f32[8,256]{1,0:T(8,128)} %copy-done.12, f32[8,256]{1,0:T(8,128)} %copy-done.14, f32[8,256]{1,0:T(8,128)} %copy-done.15, ...), custom_call_target="tpu_custom_call" | custom-call | tf_op jit(solution)/shard_map/right_side/pallas_call | solution.py:325
  17.0 16.7 %all_to_all.30.got = f32[16,8,128]{2,1,0:T(8,128)} all-to-all(f32[16,8,128]{2,1,0:T(8,128)} %get-tuple-element.34), channel_id=1, replica_groups=mesh['row'=16,'col'=16] {'col'}, dimensions={0} | all-to-all | bytes 131072 | tf_op jit(solution)/shard_map/all_to_all | solution.py:296
  35.4 5.3 %all-to-all-start.1 = ((f32[16,8,896]{2,1,0:T(8,128)}), f32[16,8,896]{2,1,0:T(8,128)S(1)}, u32[]{:S(2)}, u32[]{:S(2)}) async-start(f32[16,8,896]{2,1,0:T(8,128)} %pack_picked.1), calls=%async_computation.1 | async-start | bytes 917504 | tf_op jit(solution)/shard_map/all_to_all | solution.py:296
  41.3 8.6 %split_matrices.1 = (bf16[1024,1024]{1,0:T(8,128)(2,1)}, bf16[1024,1024]{1,0:T(8,128)(2,1)}, bf16[1024,1024]{1,0:T(8,128)(2,1)}, bf16[1024,1024]{1,0:T(8,128)(2,...) custom-call(f32[1024,1024]{1,0:T(8,128)} %bitcast.17, f32[1024,1024]{1,0:T(8,128)} %bitcast.18, f32[48,12288]{1,0:T(8,128)} %coarse.1), custom_call_target="tpu_custom_call" | custom-call | flops 2147483648 | tf_op jit(solution)/shard_map/split_matrices/pallas_call | solution.py:318
  49.9 3.8 %first_solve.1.present = f32[8,1024]{1,0:T(8,128)} custom-call(f32[8,1024]{1,0:T(8,128)} %get-tuple-element.37.scaled, bf16[1024,1024]{1,0:T(8,128)(2,1)} %get-tuple-element.38.high.f_high, bf16[1024,1024]{1,0:T(8,128)(2,1)} %get-tuple-element.39.low.f_low), custom_call_target="tpu_custom_call" | custom-call | flops 2147483648 | tf_op jit(solution)/shard_map/first_solve/pallas_call | solution.py:328
  54.4 10.4 %coarse_solve.1 = f32[16,8,128]{2,1,0:T(8,128)} custom-call(f32[16,8,896]{2,1,0:T(8,128)} %copy-done, bf16[48,12288]{1,0:T(8,128)(2,1)} %get-tuple-element.35.high, bf16[48,12288]{1,0:T(8,128)(2,1)} %get-tuple-element.36.low), custom_call_target="tpu_custom_call" | custom-call | tf_op jit(solution)/shard_map/coarse_solve/pallas_call | solution.py:337
  64.9 3.7 %all-to-all-start.2 = ((f32[16,8,128]{2,1,0:T(8,128)}), f32[16,8,128]{2,1,0:T(8,128)S(1)}, u32[]{:S(2)}, u32[]{:S(2)}) async-start(f32[16,8,128]{2,1,0:T(8,128)} %coarse_solve.1), calls=%async_computation.2 | async-start | bytes 131072 | tf_op jit(solution)/shard_map/all_to_all | solution.py:296
  68.6 5.9 %sweep_once.2.present = f32[8,1024]{1,0:T(8,128)} custom-call(s32[1,1]{1,0:T(1,128)S(6)} %copy.11.elements, f32[8,1024]{1,0:T(8,128)} %get-tuple-element.37.scaled, f32[8,1024]{1,0:T(8,128)} %first_solve.1.present, bf16[1024,1024]{1,0:T(8,128)(2,1)} %get-tuple-element.40.s_high.high, bf16[1024,1024]{1,0:T(8,128)(2,1)} %get-tuple-element.41.s_low.low, ...), custom_call_target="tpu_custom_call" | custom-call | flops 4294967296 | tf_op jit(solution)/shard_map/sweep_once/pallas_call | solution.py:330
  74.5 1.9 %all-to-all-done.2.got = f32[16,8,128]{2,1,0:T(8,128)S(1)} async-done(((f32[16,8,128]{2,1,0:T(8,128)}), f32[16,8,128]{2,1,0:T(8,128)S(1)}, u32[]{:S(2)}, u32[]{:S(2)}) %all-to-all-start.2) | async-done | bytes 65568 | tf_op jit(solution)/shard_map/all_to_all | solution.py:296
  77.1 2.4 %pack_solved.1 = f32[16,8,128]{2,1,0:T(8,128)} custom-call(s32[2]{0:T(128)} %pad_add_fusion.place, f32[16,8,128]{2,1,0:T(8,128)} %copy-done.3, f32[16,8,896]{2,1,0:T(8,128)} %copy-done), custom_call_target="tpu_custom_call" | custom-call | tf_op jit(solution)/shard_map/pack_solved/pallas_call | solution.py:349
  79.4 6.9 %all-to-all-start.3 = ((f32[16,8,128]{2,1,0:T(8,128)}), f32[16,8,128]{2,1,0:T(8,128)S(1)}, u32[]{:S(2)}, u32[]{:S(2)}) async-start(f32[16,8,128]{2,1,0:T(8,128)} %pack_solved.1), calls=%async_computation.3 | async-start | bytes 131072 | tf_op jit(solution)/shard_map/all_to_all | solution.py:296
  86.4 5.9 %sweep_once.3.local = f32[8,1024]{1,0:T(8,128)} custom-call(s32[1,1]{1,0:T(1,128)S(6)} %copy.11.elements, f32[8,1024]{1,0:T(8,128)} %get-tuple-element.37.scaled, f32[8,1024]{1,0:T(8,128)} %sweep_once.2.present, bf16[1024,1024]{1,0:T(8,128)(2,1)} %get-tuple-element.40.s_high.high, bf16[1024,1024]{1,0:T(8,128)(2,1)} %get-tuple-element.41.s_low.low, ...), custom_call_target="tpu_custom_call" | custom-call | flops 4294967296 | tf_op jit(solution)/shard_map/sweep_once/pallas_call | solution.py:330
  93.5 2.1 %corrected.1 = (f32[8,1024]{1,0:T(8,128)}, f32[8,128]{1,0:T(8,128)}, f32[8,256]{1,0:T(8,128)}, f32[8,256]{1,0:T(8,128)}, f32[8,256]{1,0:T(8,128)}, /*index=5*/f32[8,256]{1,0:T(8,128)}) custom-call(s32[2]{0:T(128)} %pad_add_fusion.place, f32[16,8,128]{2,1,0:T(8,128)} %copy-done.2, s32[1,128]{1,0:T(1,128)} %pad.7.local_at, f32[8,1024]{1,0:T(8,128)} %sweep_once.3.local, ...), custom_call_target="tpu_custom_call" | custom-call | tf_op jit(solution)/shard_map/corrected/pallas_call | solution.py:351
  97.8 3.5 %collective-permute-start.7 = (f32[8,256]{1,0:T(8,128)}, f32[8,256]{1,0:T(8,128)S(1)}, u32[]{:S(2)}, u32[]{:S(2)}) collective-permute-start(f32[8,256]{1,0:T(8,128)} %get-tuple-element.47), channel_id=1, source_target_pairs={{16,32},{32,16},{48,64},{64,48},{80,96},{96,80},{112,128},{128,112... | collective-permute-start | bytes 24584 | tf_op jit(solution)/shard_map/ppermute | solution.py:290
  101.3 2.5 %collective-permute-done.7.g3 = f32[8,256]{1,0:T(8,128)S(1)} collective-permute-done((f32[8,256]{1,0:T(8,128)}, f32[8,256]{1,0:T(8,128)S(1)}, u32[]{:S(2)}, u32[]{:S(2)}) %collective-permute-start.7) | collective-permute-done | bytes 8224 | tf_op jit(solution)/shard_map/ppermute | solution.py:290
  104.4 4.4 %apply_operator.1 = (f32[8,1024]{1,0:T(8,128)}, f32[8,1024]{1,0:T(8,128)}, f32[8,256]{1,0:T(8,128)}, f32[8,256]{1,0:T(8,128)}, f32[8,256]{1,0:T(8,128)}, /*index=5*/f32[8,256]{1,0:T(8,128)}, f32[16,8,128]{2,1,0:T(8,128)}) custom-call(s32[2]{0:T(128)} %pad_add_fusion.place, f32[8,1024]{1,0:T(8,128)} %get-tuple-element.43.t, f32[8,256]{1,0:T(8,128)} %copy-done.4, ...), custom_call_target="tpu_custom_call" | custom-call | tf_op jit(solution)/shard_map/apply_operator/pallas_call | solution.py:355
  108.8 14.9 %all_to_all.31.got = f32[16,8,128]{2,1,0:T(8,128)} all-to-all(f32[16,8,128]{2,1,0:T(8,128)} %get-tuple-element.49), channel_id=1, replica_groups=mesh['row'=16,'col'=16] {'col'}, dimensions={0} | all-to-all | bytes 131072 | tf_op jit(solution)/shard_map/all_to_all | solution.py:296
  125.1 4.9 %all-to-all-start.5 = ((f32[16,8,128]{2,1,0:T(8,128)}), f32[16,8,128]{2,1,0:T(8,128)S(1)}, u32[]{:S(2)}, u32[]{:S(2)}) async-start(f32[16,8,128]{2,1,0:T(8,128)} %subtotal.1), calls=%async_computation.5 | async-start | bytes 131072 | tf_op jit(solution)/shard_map/all_to_all | solution.py:296
  131.4 3.9 %collective-permute-start.11 = (f32[8,256]{1,0:T(8,128)}, f32[8,256]{1,0:T(8,128)S(1)}, u32[]{:S(2)}, u32[]{:S(2)}) collective-permute-start(f32[8,256]{1,0:T(8,128)} %get-tuple-element.53), channel_id=1, source_target_pairs={{16,32},{32,16},{48,64},{64,48},{80,96},{96,80},{112,128},{128,112... | collective-permute-start | bytes 24584 | tf_op jit(solution)/shard_map/ppermute | solution.py:290
  137.7 2.4 %collective-permute-done.9.g1 = f32[8,256]{1,0:T(8,128)S(1)} collective-permute-done((f32[8,256]{1,0:T(8,128)}, f32[8,256]{1,0:T(8,128)S(1)}, u32[]{:S(2)}, u32[]{:S(2)}) %collective-permute-start.9) | collective-permute-done | bytes 8224 | tf_op jit(solution)/shard_map/ppermute | solution.py:290
  140.7 1.8 %finish.1 = (f32[8,1024]{1,0:T(8,128)}, f32[8,1024]{1,0:T(8,128)}) custom-call(s32[2]{0:T(128)} %pad_add_fusion.place, f32[16,8,128]{2,1,0:T(8,128)} %copy-done.1, f32[8,256]{1,0:T(8,128)} %copy-done.11, f32[8,256]{1,0:T(8,128)} %copy-done.13, f32[8,256]{1,0:T(8,128)} %copy-done.8, f32[8,256]{1,0:T(8,128)} %copy-done.9, s32[1,256]{1,0:T(1,128)} %bitcast.25, ...), custom_call_target="tpu_custom_call" | custom-call | tf_op jit(solution)/shard_map/finish/pallas_call | solution.py:363
  (58 shorter events, 18.3 us)
Async XLA Ops:
  3.0 10.9 %collective-permute-start = (f32[8,256]{1,0:T(8,128)}, f32[8,256]{1,0:T(8,128)S(1)}, u32[]{:S(2)}, u32[]{:S(2)}) collective-permute-start(f32[8,256]{1,0:T(8,128)} %get-tuple-element.30), channel_id=1, source_target_pairs={{0,1},{1,0},{2,3},{3,2},{4,5},{5,4},{6,7},{7,6},{8,9},{9,8},{10,11... | collective-permute-start | bytes 24584 | tf_op jit(solution)/shard_map/ppermute | solution.py:290
  6.2 7.7 %collective-permute-start.1 = (f32[8,256]{1,0:T(8,128)}, f32[8,256]{1,0:T(8,128)S(1)}, u32[]{:S(2)}, u32[]{:S(2)}) collective-permute-start(f32[8,256]{1,0:T(8,128)} %get-tuple-element.31), channel_id=1, source_target_pairs={{1,2},{2,1},{3,4},{4,3},{5,6},{6,5},{7,8},{8,7},{9,10},{10,9},{11,... | collective-permute-start | bytes 24584 | tf_op jit(solution)/shard_map/ppermute | solution.py:290
  6.2 7.7 %collective-permute-start.2 = (f32[8,256]{1,0:T(8,128)}, f32[8,256]{1,0:T(8,128)S(1)}, u32[]{:S(2)}, u32[]{:S(2)}) collective-permute-start(f32[8,256]{1,0:T(8,128)} %get-tuple-element.32), channel_id=1, source_target_pairs={{0,16},{16,0},{32,48},{48,32},{64,80},{80,64},{96,112},{112,96},{1... | collective-permute-start | bytes 24584 | tf_op jit(solution)/shard_map/ppermute | solution.py:290
  7.4 6.5 %collective-permute-start.3 = (f32[8,256]{1,0:T(8,128)}, f32[8,256]{1,0:T(8,128)S(1)}, u32[]{:S(2)}, u32[]{:S(2)}) collective-permute-start(f32[8,256]{1,0:T(8,128)} %get-tuple-element.33), channel_id=1, source_target_pairs={{16,32},{32,16},{48,64},{64,48},{80,96},{96,80},{112,128},{128,112... | collective-permute-start | bytes 24584 | tf_op jit(solution)/shard_map/ppermute | solution.py:290
  35.4 18.3 %all-to-all-start.1 = ((f32[16,8,896]{2,1,0:T(8,128)}), f32[16,8,896]{2,1,0:T(8,128)S(1)}, u32[]{:S(2)}, u32[]{:S(2)}) async-start(f32[16,8,896]{2,1,0:T(8,128)} %pack_picked.1), calls=%async_computation.1 | async-start | bytes 917504 | tf_op jit(solution)/shard_map/all_to_all | solution.py:296
  53.7 0.8 copy-start
  64.9 11.5 %all-to-all-start.2 = ((f32[16,8,128]{2,1,0:T(8,128)}), f32[16,8,128]{2,1,0:T(8,128)S(1)}, u32[]{:S(2)}, u32[]{:S(2)}) async-start(f32[16,8,128]{2,1,0:T(8,128)} %coarse_solve.1), calls=%async_computation.2 | async-start | bytes 131072 | tf_op jit(solution)/shard_map/all_to_all | solution.py:296
  79.4 13.5 %all-to-all-start.3 = ((f32[16,8,128]{2,1,0:T(8,128)}), f32[16,8,128]{2,1,0:T(8,128)S(1)}, u32[]{:S(2)}, u32[]{:S(2)}) async-start(f32[16,8,128]{2,1,0:T(8,128)} %pack_solved.1), calls=%async_computation.3 | async-start | bytes 131072 | tf_op jit(solution)/shard_map/all_to_all | solution.py:296
  95.6 5.7 %collective-permute-start.4 = (f32[8,256]{1,0:T(8,128)}, f32[8,256]{1,0:T(8,128)S(1)}, u32[]{:S(2)}, u32[]{:S(2)}) collective-permute-start(f32[8,256]{1,0:T(8,128)} %get-tuple-element.44), channel_id=1, source_target_pairs={{0,1},{1,0},{2,3},{3,2},{4,5},{5,4},{6,7},{7,6},{8,9},{9,8},{10,11... | collective-permute-start | bytes 24584 | tf_op jit(solution)/shard_map/ppermute | solution.py:290
  97.2 4.1 %collective-permute-start.5 = (f32[8,256]{1,0:T(8,128)}, f32[8,256]{1,0:T(8,128)S(1)}, u32[]{:S(2)}, u32[]{:S(2)}) collective-permute-start(f32[8,256]{1,0:T(8,128)} %get-tuple-element.45), channel_id=1, source_target_pairs={{1,2},{2,1},{3,4},{4,3},{5,6},{6,5},{7,8},{8,7},{9,10},{10,9},{11,... | collective-permute-start | bytes 24584 | tf_op jit(solution)/shard_map/ppermute | solution.py:290
  97.5 3.8 %collective-permute-start.6 = (f32[8,256]{1,0:T(8,128)}, f32[8,256]{1,0:T(8,128)S(1)}, u32[]{:S(2)}, u32[]{:S(2)}) collective-permute-start(f32[8,256]{1,0:T(8,128)} %get-tuple-element.46), channel_id=1, source_target_pairs={{0,16},{16,0},{32,48},{48,32},{64,80},{80,64},{96,112},{112,96},{1... | collective-permute-start | bytes 24584 | tf_op jit(solution)/shard_map/ppermute | solution.py:290
  97.8 6.0 %collective-permute-start.7 = (f32[8,256]{1,0:T(8,128)}, f32[8,256]{1,0:T(8,128)S(1)}, u32[]{:S(2)}, u32[]{:S(2)}) collective-permute-start(f32[8,256]{1,0:T(8,128)} %get-tuple-element.47), channel_id=1, source_target_pairs={{16,32},{32,16},{48,64},{64,48},{80,96},{96,80},{112,128},{128,112... | collective-permute-start | bytes 24584 | tf_op jit(solution)/shard_map/ppermute | solution.py:290
  101.3 2.5 %copy-start.4 = (f32[8,256]{1,0:T(8,128)}, f32[8,256]{1,0:T(8,128)S(1)}, u32[]{:S(2)}) copy-start(f32[8,256]{1,0:T(8,128)S(1)} %collective-permute-done.4.g0) | copy-start | bytes 24580
  101.3 2.5 %copy-start.5 = (f32[8,256]{1,0:T(8,128)}, f32[8,256]{1,0:T(8,128)S(1)}, u32[]{:S(2)}) copy-start(f32[8,256]{1,0:T(8,128)S(1)} %collective-permute-done.5.g1) | copy-start | bytes 24580
  101.3 2.5 %copy-start.6 = (f32[8,256]{1,0:T(8,128)}, f32[8,256]{1,0:T(8,128)S(1)}, u32[]{:S(2)}) copy-start(f32[8,256]{1,0:T(8,128)S(1)} %collective-permute-done.6.g2) | copy-start | bytes 24580
  125.1 15.0 %all-to-all-start.5 = ((f32[16,8,128]{2,1,0:T(8,128)}), f32[16,8,128]{2,1,0:T(8,128)S(1)}, u32[]{:S(2)}, u32[]{:S(2)}) async-start(f32[16,8,128]{2,1,0:T(8,128)} %subtotal.1), calls=%async_computation.5 | async-start | bytes 131072 | tf_op jit(solution)/shard_map/all_to_all | solution.py:296
  130.0 6.8 %collective-permute-start.10 = (f32[8,256]{1,0:T(8,128)}, f32[8,256]{1,0:T(8,128)S(1)}, u32[]{:S(2)}, u32[]{:S(2)}) collective-permute-start(f32[8,256]{1,0:T(8,128)} %get-tuple-element.52), channel_id=1, source_target_pairs={{0,16},{16,0},{32,48},{48,32},{64,80},{80,64},{96,112},{112,96},{1... | collective-permute-start | bytes 24584 | tf_op jit(solution)/shard_map/ppermute | solution.py:290
  131.4 6.3 %collective-permute-start.11 = (f32[8,256]{1,0:T(8,128)}, f32[8,256]{1,0:T(8,128)S(1)}, u32[]{:S(2)}, u32[]{:S(2)}) collective-permute-start(f32[8,256]{1,0:T(8,128)} %get-tuple-element.53), channel_id=1, source_target_pairs={{16,32},{32,16},{48,64},{64,48},{80,96},{96,80},{112,128},{128,112... | collective-permute-start | bytes 24584 | tf_op jit(solution)/shard_map/ppermute | solution.py:290
  135.3 2.4 %collective-permute-start.8 = (f32[8,256]{1,0:T(8,128)}, f32[8,256]{1,0:T(8,128)S(1)}, u32[]{:S(2)}, u32[]{:S(2)}) collective-permute-start(f32[8,256]{1,0:T(8,128)} %get-tuple-element.50), channel_id=1, source_target_pairs={{0,1},{1,0},{2,3},{3,2},{4,5},{5,4},{6,7},{7,6},{8,9},{9,8},{10,11... | collective-permute-start | bytes 24584 | tf_op jit(solution)/shard_map/ppermute | solution.py:290
  136.5 3.6 %collective-permute-start.9 = (f32[8,256]{1,0:T(8,128)}, f32[8,256]{1,0:T(8,128)S(1)}, u32[]{:S(2)}, u32[]{:S(2)}) collective-permute-start(f32[8,256]{1,0:T(8,128)} %get-tuple-element.51), channel_id=1, source_target_pairs={{1,2},{2,1},{3,4},{4,3},{5,6},{6,5},{7,8},{8,7},{9,10},{10,9},{11,... | collective-permute-start | bytes 24584 | tf_op jit(solution)/shard_map/ppermute | solution.py:290
  136.8 3.3 %copy-start.8 = (f32[8,256]{1,0:T(8,128)}, f32[8,256]{1,0:T(8,128)S(1)}, u32[]{:S(2)}) copy-start(f32[8,256]{1,0:T(8,128)S(1)} %collective-permute-done.10.g2) | copy-start | bytes 24580
  137.7 2.4 %copy-start.9 = (f32[8,256]{1,0:T(8,128)}, f32[8,256]{1,0:T(8,128)S(1)}, u32[]{:S(2)}) copy-start(f32[8,256]{1,0:T(8,128)S(1)} %collective-permute-done.11.g3) | copy-start | bytes 24580
  137.7 2.4 %copy-start.11 = (f32[8,256]{1,0:T(8,128)}, f32[8,256]{1,0:T(8,128)S(1)}, u32[]{:S(2)}) copy-start(f32[8,256]{1,0:T(8,128)S(1)} %collective-permute-done.8.g0) | copy-start | bytes 24580
  140.1 0.6 copy-start.1
  (8 other events, 4.8 us)

commit v2 on v1

--- a/solution.py
+++ b/solution.py
@@ -10,6 +10,8 @@
 F32, BF16 = jnp.float32, jnp.bfloat16
 VM = pl.BlockSpec(memory_space=pltpu.VMEM)
 SM = pl.BlockSpec(memory_space=pltpu.SMEM)
+HB = pl.BlockSpec(memory_space=pltpu.HBM)
+CHUNK = 256
 LANES = 128
 NPRIM = 48
 SIDE = 16
@@ -17,20 +19,43 @@
 RADIX = 256
 
 
-def call(body, outs, specs, scratch=(), flops=0, moved=0):
-    return pl.pallas_call(
+def call(body, outs, kinds, scratch=(), flops=0, room=8, grid=(), blocks={}):
+    places = {"s": SM, "v": VM, "h": VM, "b": HB}
+    kernel = pl.pallas_call(
         body,
         out_shape=outs,
-        in_specs=specs,
+        grid=grid,
+        in_specs=[blocks.get(i, places[kind]) for i, kind in enumerate(kinds)],
         out_specs=jax.tree.map(lambda _: VM, outs),
         scratch_shapes=list(scratch),
-        cost_estimate=pl.CostEstimate(flops=flops, transcendentals=0, bytes_accessed=moved),
+        cost_estimate=pl.CostEstimate(flops=flops, transcendentals=0, bytes_accessed=0),
+        compiler_params=pltpu.CompilerParams(vmem_limit_bytes=room << 20),
         name=body.__name__,
     )
 
+    def run(*args):
+        return kernel(
+            *(
+                x
+                if kind == "s"
+                else pltpu.with_memory_space_constraint(x, pltpu.VMEM if kind == "v" else pltpu.HBM)
+                for x, kind in zip(args, kinds, strict=True)
+            )
+        )
+
+    return run
+
 
 def shape(*dims, dtype=F32):
-    return jax.ShapeDtypeStruct(dims, dtype)
+    return pltpu.VMEM(dims, dtype)
+
+
+def widened(row):
+    return jnp.concatenate([row, jnp.zeros((1, LANES - row.shape[1]), row.dtype)], axis=1)
+
+
+def coordinates():
+    return lax.axis_index(ROW), lax.axis_index(COL)
 
 
 def halves(x):
@@ -109,27 +134,27 @@
     return jnp.concatenate(parts, axis=1)
 
 
-def split_matrices(schur, factor, coarse, *outs):
-    for k, ref in enumerate((schur, factor, coarse)):
-        high, low = halves(ref[...])
-        outs[2 * k][...] = high
-        outs[2 * k + 1][...] = low
-
-
-def first_sends(place, loads, west, south, *sends):
-    write_sends(loads[...], (west[...], south[...]), place[0], place[1], sends)
-
-
-def right_side(place, loads, g0, g1, g2, g3, west, south, local_at, coarse_at, b_ref, scaled_ref, slots):
-    row, col = place[0], place[1]
+def split_matrix(matrix, high_ref, low_ref):
+    high_ref[...], low_ref[...] = halves(matrix[...])
+
+
+def first_sends(loads, west, south, local_at, coarse_at, s0, s1, s2, s3, *kept):
+    row, col = coordinates()
+    for ref, value in zip(kept, (loads, west, south, local_at, coarse_at)):
+        ref[...] = value[...]
+    write_sends(loads[...], (west[...], south[...]), row, col, (s0, s1, s2, s3))
+
+
+def right_side(loads, g0, g1, g2, g3, west, south, local_at, coarse_at, b_ref, scaled_ref, slots):
+    row, col = coordinates()
     b = loads[...] + halo([g0[...], g1[...], g2[...], g3[...]], (west[...], south[...]), row, col)
     scaled = weight_row(row, col, b.shape[1]) * b
     b_ref[...] = b
     scaled_ref[...] = scaled
-    picked = selected(scaled, one_hot((b.shape[1], LANES), local_at[...]), nn)
+    picked = selected(scaled, one_hot((b.shape[1], NPRIM), local_at[...]), nn)
     lane = lax.broadcasted_iota(jnp.int32, (8, LANES), 1)
-    tile = jnp.where(lane < NPRIM, picked, 0.0)
-    index = jnp.broadcast_to(coarse_at[...].astype(F32), (8, LANES))
+    tile = jnp.concatenate([picked, jnp.zeros((8, LANES - NPRIM), F32)], axis=1)
+    index = jnp.broadcast_to(widened(coarse_at[...]).astype(F32), (8, LANES))
     index = pltpu.roll(index, IDX_AT, 1)
     tile = jnp.where((lane >= IDX_AT) & (lane < IDX_AT + NPRIM), index, tile)
     for i in range(SIDE):
@@ -154,7 +179,7 @@
     values = packed(lambda i: got[i], 0)
     index = packed(lambda i: got[i], IDX_AT)
     below = lax.broadcasted_iota(jnp.int32, (8, LANES), 0)
-    last = jnp.broadcast_to(coarse_at[...].astype(F32), (8, LANES))
+    last = jnp.broadcast_to(widened(coarse_at[...]).astype(F32), (8, LANES))
     for t, tile in enumerate(index):
         last = jnp.where(below == t, tile, last)
     for i in range(SIDE):
@@ -162,9 +187,11 @@
             slots[i, :, t * LANES : (t + 1) * LANES] = tile
 
 
-def coarse_solve(got, high, low, slots, spread, hot, total, rhs):
+def coarse_solve(got, coarse, slots, spread, hot, total, rhs, here, arrived):
     width = SIDE * NPRIM
-    blocks = high.shape[1] // RADIX
+    blocks = coarse.shape[1] // RADIX
+    copy = pltpu.make_async_copy(coarse, here, arrived)
+    copy.start()
     total[...] = jnp.zeros_like(total)
     rows16 = lax.broadcasted_iota(jnp.int32, (16, LANES), 0).astype(F32)
 
@@ -201,15 +228,18 @@
         rhs[:, l * RADIX : (l + 1) * RADIX] = jnp.concatenate(
             [v_high, value - v_high], axis=0
         ).astype(BF16)
-    first = nt(rhs[...], high[...])
-    second = nt(rhs[...], low[...])
+    copy.wait()
+    high, low = halves(here[...])
+    first = nt(rhs[...], high)
+    second = nt(rhs[...], low)
     solved = first[:8] + first[8:] + second[:8]
     tile = jnp.concatenate([solved, jnp.zeros((8, LANES - NPRIM), F32)], axis=1)
     for i in range(SIDE):
         slots[i] = tile
 
 
-def pack_solved(place, got, asked, slots):
+def pack_solved(got, asked, slots):
+    row, _ = coordinates()
     width = SIDE * NPRIM
     mine = jnp.concatenate(packed(lambda i: got[i], 0), axis=1)
     parts = jnp.concatenate([p.astype(F32) for p in thirds(mine)], axis=0)
@@ -217,31 +247,34 @@
     lane = lax.broadcasted_iota(jnp.int32, (1, LANES), 1)
     for i in range(SIDE):
         want = asked[i, width // LANES : width // LANES + 1, width : width + LANES]
-        want = jnp.where(lane < NPRIM, want.astype(jnp.int32) - width * place[0], -1)
+        want = jnp.where(lane < NPRIM, want.astype(jnp.int32) - width * row, -1)
         found = nn(parts, one_hot((width, LANES), want))
         slots[i] = found[:8] + found[8:16] + found[16:24]
 
 
-def corrected(place, got, local_at, local, b, west, south, t_ref, gamma, s0, s1, s2, s3):
-    row, col = place[0], place[1]
+def corrected(got, local_at, local, b, west, south, t_ref, gamma, s0, s1, s2, s3):
+    row, col = coordinates()
     rows = got[0]
     for i in range(1, SIDE):
         rows = rows + got[i]
     unknowns = local.shape[1]
-    lane = lax.broadcasted_iota(jnp.int32, (8, LANES), 1)
-    rows = jnp.where(lane < NPRIM, rows, 0.0)
-    correction = selected(rows, one_hot((unknowns, LANES), local_at[...]), nt)
+    correction = selected(rows[:, :NPRIM], one_hot((unknowns, NPRIM), local_at[...]), nt)
     t = weight_row(row, col, unknowns) * (local[...] + correction)
     t_ref[...] = t
     gamma[...] = jnp.broadcast_to(jnp.sum(b[...] * t, axis=1, keepdims=True), (8, LANES))
     write_sends(t, (west[...], south[...]), row, col, (s0, s1, s2, s3))
 
 
-def apply_operator(place, t, g0, g1, g2, g3, west, south, high, low, gamma, p_ref, u_ref, s0, s1, s2, s3, slots):
-    row, col = place[0], place[1]
+def apply_operator(t, g0, g1, g2, g3, west, south, high, low, gamma, p_ref, u_ref, s0, s1, s2, s3, slots, here, arrived):
+    copy = pltpu.make_async_copy(low, here, arrived)
+    copy.start()
+    row, col = coordinates()
     orders = (west[...], south[...])
     p = t[...] + halo([g0[...], g1[...], g2[...], g3[...]], orders, row, col)
-    u = times(p, high[...], low[...])
+    p_high, p_low = halves(p)
+    u = nn(p_high, high[...]) + nn(p_low, high[...])
+    copy.wait()
+    u = u + nn(p_high, here[...])
     p_ref[...] = p
     u_ref[...] = u
     write_sends(u, orders, row, col, (s0, s1, s2, s3))
@@ -260,25 +293,46 @@
         slots[i] = tile
 
 
-def finish(place, got, g0, g1, g2, g3, west, south, p, u, b, solution_ref, residual_ref):
+def finish(got, g0, g1, g2, g3, west, south, p, u, b, solution_ref, residual_ref):
     tile = got[0]
     for i in range(1, SIDE):
         tile = tile + got[i]
+    row, col = coordinates()
     alpha = tile[:, 0:1] / tile[:, 1:2]
-    q = u[...] + halo([g0[...], g1[...], g2[...], g3[...]], (west[...], south[...]), place[0], place[1])
+    q = u[...] + halo([g0[...], g1[...], g2[...], g3[...]], (west[...], south[...]), row, col)
     solution_ref[...] = alpha * p[...]
     residual_ref[...] = b[...] - alpha * q
 
 
-def first_solve(scaled, high, low, local):
-    local[...] = times(scaled[...], high[...], low[...])
+def chunk_of(ref, k):
+    return ref[:, pl.ds(pl.multiple_of(k * CHUNK, CHUNK), CHUNK)]
+
+
+def first_solve(scaled, factor, local):
+    k = pl.program_id(0)
+    part = times(chunk_of(scaled, k), *halves(factor[...]))
+    local[...] = jnp.where(k == 0, part, local[...] + part)
 
 
 def sweep(turn):
-    def sweep_once(elements, scaled, present, s_high, s_low, f_high, f_low, local):
-        rest = scaled[...] - times(present[...], s_high[...], s_low[...])
-        after = present[...] + times(rest, f_high[...], f_low[...])
-        local[...] = jnp.where(elements[0, 0] // ELEM_BASE > turn, after, present[...])
+    def sweep_once(elements, scaled, present, schur, factor, local, rest):
+        k = pl.program_id(0)
+        half = pl.num_programs(0) // 2
+
+        @pl.when(k < half)
+        def _():
+            part = times(chunk_of(present, k), *halves(schur[...]))
+            rest[...] = jnp.where(k == 0, scaled[...], rest[...]) - part
+
+        @pl.when(k >= half)
+        def _():
+            part = times(chunk_of(rest, k - half), *halves(factor[...]))
+            local[...] = jnp.where(k == half, present[...], local[...]) + part
+
+        @pl.when(k == 2 * half - 1)
+        def _():
+            done = elements[0, 0] // ELEM_BASE <= turn
+            local[...] = jnp.where(done, present[...], local[...])
 
     return sweep_once
 
@@ -302,66 +356,102 @@
     loads_t = loads[0, 0].T
     unknowns = loads_t.shape[1]
     face = unknowns // 4
-    matrix = (unknowns, unknowns)
-    place = jnp.stack([lax.axis_index(ROW), lax.axis_index(COL)]).astype(jnp.int32)
     west, south = west_map[0], south_map[0]
-    pad = ((0, 0), (0, LANES - NPRIM))
-    local_at = jnp.pad(prim_local[0], pad, constant_values=-1)
-    coarse_at = jnp.pad(prim_coarse[0], pad)
+    local_at, coarse_at = prim_local[0], prim_coarse[0]
     field = shape(8, unknowns)
+    matrix = shape(unknowns, unknowns, dtype=BF16)
     sends_shape = [shape(8, face)] * 4
     tiles = shape(SIDE, 8, LANES)
     width = SIDE * NPRIM
     product_flops = 2 * 1024 * unknowns * unknowns
 
-    sends = call(first_sends, sends_shape, [SM] + [VM] * 3)(place, loads_t, west, south)
-    s_high, s_low, f_high, f_low, c_high, c_low = call(
-        split_matrices,
-        [shape(*matrix, dtype=BF16)] * 4 + [shape(*coarse_inverse.shape, dtype=BF16)] * 2,
-        [VM] * 3,
+    kept_shape = [
+        pltpu.VMEM(x.shape, x.dtype) for x in (loads_t, west, south, local_at, coarse_at)
+    ]
+    *sends, loads_t, west, south, local_at, coarse_at = call(
+        first_sends, sends_shape + kept_shape, "h" * 5
+    )(loads_t, west, south, local_at, coarse_at)
+    got = swapped(sends)
+    b, scaled, slots = call(right_side, [field, field, tiles], "v" * 9)(
+        loads_t, *got, west, south, local_at, coarse_at
+    )
+    steps = unknowns // CHUNK
+    strip = (CHUNK, unknowns)
+    matrices = (schur[0, 0], factor[0, 0])
+    local = call(
+        first_solve,
+        field,
+        "vh",
         flops=product_flops,
-    )(schur[0, 0], factor[0, 0], coarse_inverse)
-    got = swapped(sends)
-    b, scaled, slots = call(right_side, [field, field, tiles], [SM] + [VM] * 9)(
-        place, loads_t, *got, west, south, local_at, coarse_at
-    )
-    local = call(first_solve, field, [VM] * 3, flops=product_flops)(scaled, f_high, f_low)
-    for turn in (1, 2):
-        local = call(sweep(turn), field, [SM] + [VM] * 6, flops=2 * product_flops)(
-            elements, scaled, local, s_high, s_low, f_high, f_low
-        )
+        grid=(steps,),
+        blocks={1: pl.BlockSpec(strip, lambda k: (k, 0))},
+    )(scaled, matrices[1])
     gathered = across(slots, COL)
-    slots = call(pack_picked, shape(SIDE, 8, width + LANES), [VM] * 2)(gathered, coarse_at)
+    gathered, local = lax.optimization_barrier((gathered, local))
+    slots = call(pack_picked, shape(SIDE, 8, width + LANES), "vv")(gathered, coarse_at)
+
+    def swept(turn, local):
+        return call(
+            sweep(turn),
+            field,
+            "svvhh",
+            scratch=(pltpu.VMEM((8, unknowns), F32),),
+            flops=2 * product_flops,
+            grid=(2 * steps,),
+            blocks={
+                3: pl.BlockSpec(strip, lambda k: (jnp.minimum(k, steps - 1), 0)),
+                4: pl.BlockSpec(strip, lambda k: (jnp.maximum(k - steps, 0), 0)),
+            },
+        )(elements, scaled, local, *matrices)
+
+    local = swept(1, local)
     asked = across(slots, ROW)
-    rows = 16 * coarse_inverse.shape[1] // RADIX
+    asked, local = lax.optimization_barrier((asked, local))
+    hot_rows = 16 * coarse_inverse.shape[1] // RADIX
     slots = call(
         coarse_solve,
         tiles,
-        [VM] * 3,
+        "vb",
+        room=20,
         scratch=(
-            pltpu.VMEM((rows, 2 * width), BF16),
+            pltpu.VMEM((hot_rows, 2 * width), BF16),
             pltpu.VMEM((RADIX, 2 * width), BF16),
-            pltpu.VMEM((rows, RADIX), F32),
+            pltpu.VMEM((hot_rows, RADIX), F32),
             pltpu.VMEM((16, coarse_inverse.shape[1]), BF16),
+            pltpu.VMEM(coarse_inverse.shape, F32),
+            pltpu.SemaphoreType.DMA,
         ),
-    )(asked, c_high, c_low)
+    )(asked, coarse_inverse)
     gathered = across(slots, COL)
-    slots = call(pack_solved, tiles, [SM] + [VM] * 2)(place, gathered, asked)
+    local = swept(2, local)
+    gathered, local = lax.optimization_barrier((gathered, local))
+    slots = call(pack_solved, tiles, "vv")(gathered, asked)
     gathered = across(slots, ROW)
-    t, gamma, *sends = call(corrected, [field, shape(8, LANES)] + sends_shape, [SM] + [VM] * 6)(
-        place, gathered, local_at, local, b, west, south
+    source, _ = lax.optimization_barrier((matrices[0], local))
+    high, low = call(
+        split_matrix,
+        [matrix, jax.ShapeDtypeStruct((unknowns, unknowns), BF16)],
+        "h",
+        flops=product_flops,
+        room=12,
+    )(source)
+    gathered, high, low = lax.optimization_barrier((gathered, high, low))
+    t, gamma, *sends = call(corrected, [field, shape(8, LANES)] + sends_shape, "v" * 6)(
+        gathered, local_at, local, b, west, south
     )
     got = swapped(sends)
-    p, u, *rest = call(
-        apply_operator, [field, field] + sends_shape + [tiles], [SM] + [VM] * 10
-    )(place, t, *got, west, south, s_high, s_low, gamma)
+    p, u, *rest = call(apply_operator, [field, field] + sends_shape + [tiles], "v" * 8 + "bv", room=12,
+        scratch=(pltpu.VMEM((unknowns, unknowns), BF16), pltpu.SemaphoreType.DMA),
+    )(t, *got, west, south, high, low, gamma)
     sends, slots = rest[:4], rest[4]
     got = swapped(sends)
     gathered = across(slots, COL)
-    slots = call(subtotal, tiles, [VM])(gathered)
+    gathered, got[0], got[1] = lax.optimization_barrier((gathered, got[0], got[1]))
+    slots = call(subtotal, tiles, "v")(gathered)
     gathered = across(slots, ROW)
-    solution, residual = call(finish, [field, field], [SM] + [VM] * 10)(
-        place, gathered, *got, west, south, p, u, b
+    whole = jax.ShapeDtypeStruct((8, unknowns), F32)
+    solution, residual = call(finish, [whole, whole], "v" * 10)(
+        gathered, *got, west, south, p, u, b
     )
     return solution.T[None, None], residual.T[None, None]
 

time: 143 us -> 120 us (0.84)
  blocking collectives: 31.5 us -> 0 us
  waiting for transfers between devices: 8.35 us -> 23.3 us
  Pallas kernels: 52.1 us -> 38.7 us
  starting transfers between devices: 41.8 us -> 54.4 us
  local copies, waits for them, and re-layouts: 6.77 us -> 1.35 us
    all_to_all x2 -> x0, blocking collectives: 31.5 us -> none  [across(): return lax.all_to_all(slots, axis, split_axis=0, concat_axis=0, tiled=True)]
    all_to_all x4 -> x6, starting transfers between devices: 20.8 us -> 34.5 us  [across(): return lax.all_to_all(slots, axis, split_axis=0, concat_axis=0, tiled=True)]
    pallas_call x13, Pallas kernels: 52.1 us -> 38.7 us  [run(): kernel(*(x if kind == 's' else pltpu.with_memory_space_constraint(x, pltp...]
    all_to_all x4 -> x6, waiting for transfers between devices: 2.53 us -> 13.3 us  [across(): return lax.all_to_all(slots, axis, split_axis=0, concat_axis=0, tiled=True)]
    ppermute x12, waiting for transfers between devices: 5.82 us -> 10.1 us  [swapped(): lax.ppermute(x, axis, pairs)]
    unnamed x32 -> x2, local copies, waits for them, and re-layouts: 4.39 us -> 1.35 us
    pad x2 -> x0, local copies, waits for them, and re-layouts: 2.38 us -> none  [the longest x1 1.19 us: body(): local_at = jnp.pad(prim_local[0], pad, constant_values=-1)]
  transfers between devices with their start and end apart: 16 -> 18, of which waited for: 5 -> 11; matrix products, arithmetic and copies ran while one was open for 2% -> 0% of each run, Pallas kernels for 17% -> 17%
where the time goes in v2:
time: 120 us; the launch traced here: 119 us
  starting transfers between devices  54.4 us (45%)
  Pallas kernels  38.7 us (32%)
  waiting for transfers between devices  23.3 us (19%)
  between operations  1.37 us (1%)
  local copies, waits for them, and re-layouts  1.35 us (1%)
    pallas_call x13, Pallas kernels, run(): kernel(*(x if kind == 's' else pltpu.with_memory_space_constraint(x, pltp...  38.7 us
    all_to_all x6, starting transfers between devices, across(): return lax.all_to_all(slots, axis, split_axis=0, concat_axis=0, tiled=True)  34.5 us
    ppermute x12, starting transfers between devices, swapped(): lax.ppermute(x, axis, pairs)  19.8 us
    all_to_all x6, waiting for transfers between devices, across(): return lax.all_to_all(slots, axis, split_axis=0, concat_axis=0, tiled=True)  13.3 us
    ppermute x12, waiting for transfers between devices, swapped(): lax.ppermute(x, axis, pairs)  10.1 us
  transfers between devices with their start and end apart: 18, of which 11 were waited for; matrix products, arithmetic and copies ran while one was open for 0% of the time, Pallas kernels for 17%

profile of v2, /device:TPU:1, one launch (start us, length us, event | category | flops | bytes accessed | tf_op | source)
XLA Modules:
  0.0 119.2 jit_solution(12779993693283758976)
XLA Ops:
  1.8 3.2 %collective-permute-start = (f32[8,256]{1,0:T(8,128)S(1)}, f32[8,256]{1,0:T(8,128)S(1)}, u32[]{:S(2)}, u32[]{:S(2)}) collective-permute-start(f32[8,256]{1,0:T(8,128)S(1)} %get-tuple-element.45), channel_id=1, source_target_pairs={{0,1},{1,0},{2,3},{3,2},{4,5},{5,4},{6,7},{7,6},{8,9},{9,8},{10,11... | collective-permute-start | bytes 24584 | tf_op jit(solution)/shard_map/ppermute | solution.py:344
  6.2 4.1 %collective-permute-start.3 = (f32[8,256]{1,0:T(8,128)S(1)}, f32[8,256]{1,0:T(8,128)S(1)}, u32[]{:S(2)}, u32[]{:S(2)}) collective-permute-start(f32[8,256]{1,0:T(8,128)S(1)} %get-tuple-element.48), channel_id=1, source_target_pairs={{16,32},{32,16},{48,64},{64,48},{80,96},{96,80},{112,128},{128,112... | collective-permute-start | bytes 24584 | tf_op jit(solution)/shard_map/ppermute | solution.py:344
  10.3 1.7 %collective-permute-done.3.g3 = f32[8,256]{1,0:T(8,128)S(1)} collective-permute-done((f32[8,256]{1,0:T(8,128)S(1)}, f32[8,256]{1,0:T(8,128)S(1)}, u32[]{:S(2)}, u32[]{:S(2)}) %collective-permute-start.3) | collective-permute-done | bytes 8224 | tf_op jit(solution)/shard_map/ppermute | solution.py:344
  13.1 9.1 %all-to-all-start = ((f32[16,8,128]{2,1,0:T(8,128)}), f32[16,8,128]{2,1,0:T(8,128)S(1)}, u32[]{:S(2)}, u32[]{:S(2)}) async-start(f32[16,8,128]{2,1,0:T(8,128)} %get-tuple-element.53), calls=%async_computation | async-start | bytes 131072 | tf_op jit(solution)/shard_map/all_to_all | solution.py:350
  22.1 3.5 %first_solve.1.present = f32[8,1024]{1,0:T(8,128)S(1)} custom-call(f32[8,1024]{1,0:T(8,128)S(1)} %get-tuple-element.54.scaled, f32[1024,1024]{1,0:T(8,128)} %bitcast.20), custom_call_target="tpu_custom_call" | custom-call | flops 2147483648 | tf_op jit(solution)/shard_map/first_solve/pallas_call | solution.py:37
  25.7 4.3 %all-to-all-done.got = f32[16,8,128]{2,1,0:T(8,128)S(1)} async-done(((f32[16,8,128]{2,1,0:T(8,128)}), f32[16,8,128]{2,1,0:T(8,128)S(1)}, u32[]{:S(2)}, u32[]{:S(2)}) %all-to-all-start) | async-done | bytes 65568 | tf_op jit(solution)/shard_map/all_to_all | solution.py:350
  30.9 5.5 %all-to-all-start.1 = ((f32[16,8,896]{2,1,0:T(8,128)}), f32[16,8,896]{2,1,0:T(8,128)S(1)}, u32[]{:S(2)}, u32[]{:S(2)}) async-start(f32[16,8,896]{2,1,0:T(8,128)} %pack_picked.1), calls=%async_computation.1 | async-start | bytes 917504 | tf_op jit(solution)/shard_map/all_to_all | solution.py:350
  37.0 7.0 %sweep_once.2.present = f32[8,1024]{1,0:T(8,128)S(1)} custom-call(s32[1,1]{1,0:T(1,128)S(6)} %copy.11.elements, f32[8,1024]{1,0:T(8,128)S(1)} %get-tuple-element.54.scaled, f32[8,1024]{1,0:T(8,128)S(1)} %first_solve.1.present, f32[1024,1024]{1,0:T(8,128)} %bitcast.23, f32[1024,1024]{1,0:T(8,128)} %bitcast.21), custom_call_target="tpu_custom_call" | custom-call | flops 4294967296 | tf_op jit(solution)/shard_map/sweep_once/pallas_call | solution.py:37
  44.0 2.1 %all-to-all-done.1.got.asked = f32[16,8,896]{2,1,0:T(8,128)S(1)} async-done(((f32[16,8,896]{2,1,0:T(8,128)}), f32[16,8,896]{2,1,0:T(8,128)S(1)}, u32[]{:S(2)}, u32[]{:S(2)}) %all-to-all-start.1) | async-done | bytes 458784 | tf_op jit(solution)/shard_map/all_to_all | solution.py:350
  46.1 8.7 %coarse_solve.1 = f32[16,8,128]{2,1,0:T(8,128)} custom-call(f32[16,8,896]{2,1,0:T(8,128)S(1)} %all-to-all-done.1.got.asked, f32[48,12288]{1,0:T(8,128)} %coarse.1), custom_call_target="tpu_custom_call" | custom-call | tf_op jit(solution)/shard_map/coarse_solve/pallas_call | solution.py:37
  54.8 5.3 %all-to-all-start.2 = ((f32[16,8,128]{2,1,0:T(8,128)}), f32[16,8,128]{2,1,0:T(8,128)S(1)}, u32[]{:S(2)}, u32[]{:S(2)}) async-start(f32[16,8,128]{2,1,0:T(8,128)} %coarse_solve.1), calls=%async_computation.2 | async-start | bytes 131072 | tf_op jit(solution)/shard_map/all_to_all | solution.py:350
  60.1 7.0 %sweep_once.3.local = f32[8,1024]{1,0:T(8,128)S(1)} custom-call(s32[1,1]{1,0:T(1,128)S(6)} %copy.11.elements, f32[8,1024]{1,0:T(8,128)S(1)} %get-tuple-element.54.scaled, f32[8,1024]{1,0:T(8,128)S(1)} %sweep_once.2.present, f32[1024,1024]{1,0:T(8,128)} %bitcast.24, f32[1024,1024]{1,0:T(8,128)} %bitcast.22), custom_call_target="tpu_custom_call" | custom-call | flops 4294967296 | tf_op jit(solution)/shard_map/sweep_once/pallas_call | solution.py:37
  69.2 3.5 %all-to-all-start.3 = ((f32[16,8,128]{2,1,0:T(8,128)}), f32[16,8,128]{2,1,0:T(8,128)S(1)}, u32[]{:S(2)}, u32[]{:S(2)}) async-start(f32[16,8,128]{2,1,0:T(8,128)} %pack_solved.1), calls=%async_computation.3 | async-start | bytes 131072 | tf_op jit(solution)/shard_map/all_to_all | solution.py:350
  72.8 2.9 %split_matrix.1 = (bf16[1024,1024]{1,0:T(8,128)(2,1)S(1)}, bf16[1024,1024]{1,0:T(8,128)(2,1)S(1)}) custom-call(f32[1024,1024]{1,0:T(8,128)} %bitcast.25), custom_call_target="tpu_custom_call" | custom-call | flops 2147483648 | tf_op jit(solution)/shard_map/split_matrix/pallas_call | solution.py:37
  77.0 2.2 %all-to-all-done.3.got = f32[16,8,128]{2,1,0:T(8,128)S(1)} async-done(((f32[16,8,128]{2,1,0:T(8,128)}), f32[16,8,128]{2,1,0:T(8,128)S(1)}, u32[]{:S(2)}, u32[]{:S(2)}) %all-to-all-start.3) | async-done | bytes 65568 | tf_op jit(solution)/shard_map/all_to_all | solution.py:350
  82.3 1.8 %collective-permute-start.7 = (f32[8,256]{1,0:T(8,128)S(1)}, f32[8,256]{1,0:T(8,128)S(1)}, u32[]{:S(2)}, u32[]{:S(2)}) collective-permute-start(f32[8,256]{1,0:T(8,128)S(1)} %get-tuple-element.70), channel_id=1, source_target_pairs={{16,32},{32,16},{48,64},{64,48},{80,96},{96,80},{112,128},{128,112... | collective-permute-start | bytes 24584 | tf_op jit(solution)/shard_map/ppermute | solution.py:344
  84.8 3.3 %collective-permute-done.7.g3 = f32[8,256]{1,0:T(8,128)S(1)} collective-permute-done((f32[8,256]{1,0:T(8,128)S(1)}, f32[8,256]{1,0:T(8,128)S(1)}, u32[]{:S(2)}, u32[]{:S(2)}) %collective-permute-start.7) | collective-permute-done | bytes 8224 | tf_op jit(solution)/shard_map/ppermute | solution.py:344
  88.1 3.2 %apply_operator.1 = (f32[8,1024]{1,0:T(8,128)S(1)}, f32[8,1024]{1,0:T(8,128)S(1)}, f32[8,256]{1,0:T(8,128)S(1)}, f32[8,256]{1,0:T(8,128)S(1)}, f32[8,256]{1,0:T(...) custom-call(f32[8,1024]{1,0:T(8,128)S(1)} %get-tuple-element.66.t, f32[8,256]{1,0:T(8,128)S(1)} %collective-permute-done.4.g0, ...), custom_call_target="tpu_custom_call" | custom-call | tf_op jit(solution)/shard_map/apply_operator/pallas_call | solution.py:37
  91.3 7.7 %all-to-all-start.4 = ((f32[16,8,128]{2,1,0:T(8,128)}), f32[16,8,128]{2,1,0:T(8,128)S(1)}, u32[]{:S(2)}, u32[]{:S(2)}) async-start(f32[16,8,128]{2,1,0:T(8,128)} %get-tuple-element.74), calls=%async_computation.4 | async-start | bytes 131072 | tf_op jit(solution)/shard_map/all_to_all | solution.py:350
  100.7 2.2 %collective-permute-done.9.g1 = f32[8,256]{1,0:T(8,128)S(1)} collective-permute-done((f32[8,256]{1,0:T(8,128)S(1)}, f32[8,256]{1,0:T(8,128)S(1)}, u32[]{:S(2)}, u32[]{:S(2)}) %collective-permute-start.9) | collective-permute-done | bytes 8224 | tf_op jit(solution)/shard_map/ppermute | solution.py:344
  102.9 3.9 %all-to-all-done.4.got = f32[16,8,128]{2,1,0:T(8,128)S(1)} async-done(((f32[16,8,128]{2,1,0:T(8,128)}), f32[16,8,128]{2,1,0:T(8,128)S(1)}, u32[]{:S(2)}, u32[]{:S(2)}) %all-to-all-start.4) | async-done | bytes 65568 | tf_op jit(solution)/shard_map/all_to_all | solution.py:350
  107.5 3.5 %all-to-all-start.5 = ((f32[16,8,128]{2,1,0:T(8,128)}), f32[16,8,128]{2,1,0:T(8,128)S(1)}, u32[]{:S(2)}, u32[]{:S(2)}) async-start(f32[16,8,128]{2,1,0:T(8,128)} %subtotal.1), calls=%async_computation.5 | async-start | bytes 131072 | tf_op jit(solution)/shard_map/all_to_all | solution.py:350
  112.2 4.0 %collective-permute-start.11 = (f32[8,256]{1,0:T(8,128)S(1)}, f32[8,256]{1,0:T(8,128)S(1)}, u32[]{:S(2)}, u32[]{:S(2)}) collective-permute-start(f32[8,256]{1,0:T(8,128)S(1)} %get-tuple-element.81), channel_id=1, source_target_pairs={{16,32},{32,16},{48,64},{64,48},{80,96},{96,80},{112,128},{128,112... | collective-permute-start | bytes 24584 | tf_op jit(solution)/shard_map/ppermute | solution.py:344
  116.2 2.1 %collective-permute-done.11.g3 = f32[8,256]{1,0:T(8,128)S(1)} collective-permute-done((f32[8,256]{1,0:T(8,128)S(1)}, f32[8,256]{1,0:T(8,128)S(1)}, u32[]{:S(2)}, u32[]{:S(2)}) %collective-permute-start.11) | collective-permute-done | bytes 8224 | tf_op jit(solution)/shard_map/ppermute | solution.py:344
  (27 shorter events, 16.0 us)
Async XLA Ops:
  1.8 8.5 %collective-permute-start = (f32[8,256]{1,0:T(8,128)S(1)}, f32[8,256]{1,0:T(8,128)S(1)}, u32[]{:S(2)}, u32[]{:S(2)}) collective-permute-start(f32[8,256]{1,0:T(8,128)S(1)} %get-tuple-element.45), channel_id=1, source_target_pairs={{0,1},{1,0},{2,3},{3,2},{4,5},{5,4},{6,7},{7,6},{8,9},{9,8},{10,11... | collective-permute-start | bytes 24584 | tf_op jit(solution)/shard_map/ppermute | solution.py:344
  5.0 5.3 %collective-permute-start.1 = (f32[8,256]{1,0:T(8,128)S(1)}, f32[8,256]{1,0:T(8,128)S(1)}, u32[]{:S(2)}, u32[]{:S(2)}) collective-permute-start(f32[8,256]{1,0:T(8,128)S(1)} %get-tuple-element.46), channel_id=1, source_target_pairs={{1,2},{2,1},{3,4},{4,3},{5,6},{6,5},{7,8},{8,7},{9,10},{10,9},{11,... | collective-permute-start | bytes 24584 | tf_op jit(solution)/shard_map/ppermute | solution.py:344
  5.0 5.3 %collective-permute-start.2 = (f32[8,256]{1,0:T(8,128)S(1)}, f32[8,256]{1,0:T(8,128)S(1)}, u32[]{:S(2)}, u32[]{:S(2)}) collective-permute-start(f32[8,256]{1,0:T(8,128)S(1)} %get-tuple-element.47), channel_id=1, source_target_pairs={{0,16},{16,0},{32,48},{48,32},{64,80},{80,64},{96,112},{112,96},{1... | collective-permute-start | bytes 24584 | tf_op jit(solution)/shard_map/ppermute | solution.py:344
  6.2 5.8 %collective-permute-start.3 = (f32[8,256]{1,0:T(8,128)S(1)}, f32[8,256]{1,0:T(8,128)S(1)}, u32[]{:S(2)}, u32[]{:S(2)}) collective-permute-start(f32[8,256]{1,0:T(8,128)S(1)} %get-tuple-element.48), channel_id=1, source_target_pairs={{16,32},{32,16},{48,64},{64,48},{80,96},{96,80},{112,128},{128,112... | collective-permute-start | bytes 24584 | tf_op jit(solution)/shard_map/ppermute | solution.py:344
  13.1 16.9 %all-to-all-start = ((f32[16,8,128]{2,1,0:T(8,128)}), f32[16,8,128]{2,1,0:T(8,128)S(1)}, u32[]{:S(2)}, u32[]{:S(2)}) async-start(f32[16,8,128]{2,1,0:T(8,128)} %get-tuple-element.53), calls=%async_computation | async-start | bytes 131072 | tf_op jit(solution)/shard_map/all_to_all | solution.py:350
  30.9 15.2 %all-to-all-start.1 = ((f32[16,8,896]{2,1,0:T(8,128)}), f32[16,8,896]{2,1,0:T(8,128)S(1)}, u32[]{:S(2)}, u32[]{:S(2)}) async-start(f32[16,8,896]{2,1,0:T(8,128)} %pack_picked.1), calls=%async_computation.1 | async-start | bytes 917504 | tf_op jit(solution)/shard_map/all_to_all | solution.py:350
  54.8 13.1 %all-to-all-start.2 = ((f32[16,8,128]{2,1,0:T(8,128)}), f32[16,8,128]{2,1,0:T(8,128)S(1)}, u32[]{:S(2)}, u32[]{:S(2)}) async-start(f32[16,8,128]{2,1,0:T(8,128)} %coarse_solve.1), calls=%async_computation.2 | async-start | bytes 131072 | tf_op jit(solution)/shard_map/all_to_all | solution.py:350
  69.2 10.0 %all-to-all-start.3 = ((f32[16,8,128]{2,1,0:T(8,128)}), f32[16,8,128]{2,1,0:T(8,128)S(1)}, u32[]{:S(2)}, u32[]{:S(2)}) async-start(f32[16,8,128]{2,1,0:T(8,128)} %pack_solved.1), calls=%async_computation.3 | async-start | bytes 131072 | tf_op jit(solution)/shard_map/all_to_all | solution.py:350
  75.6 1.4 %copy-start = (bf16[1024,1024]{1,0:T(8,128)(2,1)}, bf16[1024,1024]{1,0:T(8,128)(2,1)S(1)}, u32[]{:S(2)}) copy-start(bf16[1024,1024]{1,0:T(8,128)(2,1)S(1)} %get-tuple-element.72.low) | copy-start | bytes 6291460
  79.8 4.4 %collective-permute-start.4 = (f32[8,256]{1,0:T(8,128)S(1)}, f32[8,256]{1,0:T(8,128)S(1)}, u32[]{:S(2)}, u32[]{:S(2)}) collective-permute-start(f32[8,256]{1,0:T(8,128)S(1)} %get-tuple-element.67), channel_id=1, source_target_pairs={{0,1},{1,0},{2,3},{3,2},{4,5},{5,4},{6,7},{7,6},{8,9},{9,8},{10,11... | collective-permute-start | bytes 24584 | tf_op jit(solution)/shard_map/ppermute | solution.py:344
  81.3 3.4 %collective-permute-start.5 = (f32[8,256]{1,0:T(8,128)S(1)}, f32[8,256]{1,0:T(8,128)S(1)}, u32[]{:S(2)}, u32[]{:S(2)}) collective-permute-start(f32[8,256]{1,0:T(8,128)S(1)} %get-tuple-element.68), channel_id=1, source_target_pairs={{1,2},{2,1},{3,4},{4,3},{5,6},{6,5},{7,8},{8,7},{9,10},{10,9},{11,... | collective-permute-start | bytes 24584 | tf_op jit(solution)/shard_map/ppermute | solution.py:344
  82.0 2.8 %collective-permute-start.6 = (f32[8,256]{1,0:T(8,128)S(1)}, f32[8,256]{1,0:T(8,128)S(1)}, u32[]{:S(2)}, u32[]{:S(2)}) collective-permute-start(f32[8,256]{1,0:T(8,128)S(1)} %get-tuple-element.69), channel_id=1, source_target_pairs={{0,16},{16,0},{32,48},{48,32},{64,80},{80,64},{96,112},{112,96},{1... | collective-permute-start | bytes 24584 | tf_op jit(solution)/shard_map/ppermute | solution.py:344
  82.3 5.8 %collective-permute-start.7 = (f32[8,256]{1,0:T(8,128)S(1)}, f32[8,256]{1,0:T(8,128)S(1)}, u32[]{:S(2)}, u32[]{:S(2)}) collective-permute-start(f32[8,256]{1,0:T(8,128)S(1)} %get-tuple-element.70), channel_id=1, source_target_pairs={{16,32},{32,16},{48,64},{64,48},{80,96},{96,80},{112,128},{128,112... | collective-permute-start | bytes 24584 | tf_op jit(solution)/shard_map/ppermute | solution.py:344
  91.3 15.6 %all-to-all-start.4 = ((f32[16,8,128]{2,1,0:T(8,128)}), f32[16,8,128]{2,1,0:T(8,128)S(1)}, u32[]{:S(2)}, u32[]{:S(2)}) async-start(f32[16,8,128]{2,1,0:T(8,128)} %get-tuple-element.74), calls=%async_computation.4 | async-start | bytes 131072 | tf_op jit(solution)/shard_map/all_to_all | solution.py:350
  98.9 1.8 %collective-permute-start.8 = (f32[8,256]{1,0:T(8,128)S(1)}, f32[8,256]{1,0:T(8,128)S(1)}, u32[]{:S(2)}, u32[]{:S(2)}) collective-permute-start(f32[8,256]{1,0:T(8,128)S(1)} %get-tuple-element.75), channel_id=1, source_target_pairs={{0,1},{1,0},{2,3},{3,2},{4,5},{5,4},{6,7},{7,6},{8,9},{9,8},{10,11... | collective-permute-start | bytes 24584 | tf_op jit(solution)/shard_map/ppermute | solution.py:344
  99.1 3.8 %collective-permute-start.9 = (f32[8,256]{1,0:T(8,128)S(1)}, f32[8,256]{1,0:T(8,128)S(1)}, u32[]{:S(2)}, u32[]{:S(2)}) collective-permute-start(f32[8,256]{1,0:T(8,128)S(1)} %get-tuple-element.76), channel_id=1, source_target_pairs={{1,2},{2,1},{3,4},{4,3},{5,6},{6,5},{7,8},{8,7},{9,10},{10,9},{11,... | collective-permute-start | bytes 24584 | tf_op jit(solution)/shard_map/ppermute | solution.py:344
  107.5 10.9 %all-to-all-start.5 = ((f32[16,8,128]{2,1,0:T(8,128)}), f32[16,8,128]{2,1,0:T(8,128)S(1)}, u32[]{:S(2)}, u32[]{:S(2)}) async-start(f32[16,8,128]{2,1,0:T(8,128)} %subtotal.1), calls=%async_computation.5 | async-start | bytes 131072 | tf_op jit(solution)/shard_map/all_to_all | solution.py:350
  111.0 5.2 %collective-permute-start.10 = (f32[8,256]{1,0:T(8,128)S(1)}, f32[8,256]{1,0:T(8,128)S(1)}, u32[]{:S(2)}, u32[]{:S(2)}) collective-permute-start(f32[8,256]{1,0:T(8,128)S(1)} %get-tuple-element.80), channel_id=1, source_target_pairs={{0,16},{16,0},{32,48},{48,32},{64,80},{80,64},{96,112},{112,96},{1... | collective-permute-start | bytes 24584 | tf_op jit(solution)/shard_map/ppermute | solution.py:344
  112.2 6.1 %collective-permute-start.11 = (f32[8,256]{1,0:T(8,128)S(1)}, f32[8,256]{1,0:T(8,128)S(1)}, u32[]{:S(2)}, u32[]{:S(2)}) collective-permute-start(f32[8,256]{1,0:T(8,128)S(1)} %get-tuple-element.81), channel_id=1, source_target_pairs={{16,32},{32,16},{48,64},{64,48},{80,96},{96,80},{112,128},{128,112... | collective-permute-start | bytes 24584 | tf_op jit(solution)/shard_map/ppermute | solution.py:344

commit v3 on v2

--- a/solution.py
+++ b/solution.py
@@ -19,13 +19,12 @@
 RADIX = 256
 
 
-def call(body, outs, kinds, scratch=(), flops=0, room=8, grid=(), blocks={}):
+def call(body, outs, kinds, scratch=(), flops=0, room=8):
     places = {"s": SM, "v": VM, "h": VM, "b": HB}
     kernel = pl.pallas_call(
         body,
         out_shape=outs,
-        grid=grid,
-        in_specs=[blocks.get(i, places[kind]) for i, kind in enumerate(kinds)],
+        in_specs=[places[kind] for kind in kinds],
         out_specs=jax.tree.map(lambda _: VM, outs),
         scratch_shapes=list(scratch),
         cost_estimate=pl.CostEstimate(flops=flops, transcendentals=0, bytes_accessed=0),
@@ -304,42 +303,49 @@
     residual_ref[...] = b[...] - alpha * q
 
 
-def chunk_of(ref, k):
-    return ref[:, pl.ds(pl.multiple_of(k * CHUNK, CHUNK), CHUNK)]
-
-
-def first_solve(scaled, factor, local):
-    k = pl.program_id(0)
-    part = times(chunk_of(scaled, k), *halves(factor[...]))
-    local[...] = jnp.where(k == 0, part, local[...] + part)
+def strips(matrices, here, arrived):
+    count = matrices[0].shape[0] // CHUNK
+    copies = []
+    for i, matrix in enumerate(matrices):
+        for k in range(count):
+            at = i * count + k
+            copies.append(
+                pltpu.make_async_copy(
+                    matrix.at[pl.ds(k * CHUNK, CHUNK)], here.at[at], arrived.at[at]
+                )
+            )
+    for copy in copies:
+        copy.start()
+
+    def product(i, x):
+        total = None
+        for k in range(count):
+            at = i * count + k
+            copies[at].wait()
+            part = times(x[:, k * CHUNK : (k + 1) * CHUNK], *halves(here[at]))
+            total = part if total is None else total + part
+        return total
+
+    return product
+
+
+def first_solve(scaled, factor, local, here, arrived):
+    local[...] = strips((factor,), here, arrived)(0, scaled[...])
 
 
 def sweep(turn):
-    def sweep_once(elements, scaled, present, schur, factor, local, rest):
-        k = pl.program_id(0)
-        half = pl.num_programs(0) // 2
-
-        @pl.when(k < half)
-        def _():
-            part = times(chunk_of(present, k), *halves(schur[...]))
-            rest[...] = jnp.where(k == 0, scaled[...], rest[...]) - part
-
-        @pl.when(k >= half)
-        def _():
-            part = times(chunk_of(rest, k - half), *halves(factor[...]))
-            local[...] = jnp.where(k == half, present[...], local[...]) + part
-
-        @pl.when(k == 2 * half - 1)
-        def _():
-            done = elements[0, 0] // ELEM_BASE <= turn
-            local[...] = jnp.where(done, present[...], local[...])
+    def sweep_once(elements, scaled, present, schur, factor, local, here, arrived):
+        product = strips((schur, factor), here, arrived)
+        before = present[...]
+        after = before + product(1, scaled[...] - product(0, before))
+        local[...] = jnp.where(elements[0, 0] // ELEM_BASE > turn, after, before)
 
     return sweep_once
 
 
 def swapped(sends):
     even = [(i, i ^ 1) for i in range(SIDE)]
-    odd = [(i, ((i + 1) ^ 1) - 1) for i in range(1, SIDE - 1)] + [(0, SIDE - 1), (SIDE - 1, 0)]
+    odd = [(i, ((i + 1) ^ 1) - 1) for i in range(1, SIDE - 1)]
     return [
         lax.ppermute(x, axis, pairs)
         for x, axis, pairs in zip(sends, (COL, COL, ROW, ROW), (even, odd, even, odd))
@@ -376,15 +382,18 @@
         loads_t, *got, west, south, local_at, coarse_at
     )
     steps = unknowns // CHUNK
-    strip = (CHUNK, unknowns)
+
+    def landing(count):
+        return pltpu.VMEM((count, CHUNK, unknowns), F32), pltpu.SemaphoreType.DMA((count,))
+
     matrices = (schur[0, 0], factor[0, 0])
     local = call(
         first_solve,
         field,
-        "vh",
+        "vb",
         flops=product_flops,
-        grid=(steps,),
-        blocks={1: pl.BlockSpec(strip, lambda k: (k, 0))},
+        room=12,
+        scratch=landing(steps),
     )(scaled, matrices[1])
     gathered = across(slots, COL)
     gathered, local = lax.optimization_barrier((gathered, local))
@@ -394,14 +403,10 @@
         return call(
             sweep(turn),
             field,
-            "svvhh",
-            scratch=(pltpu.VMEM((8, unknowns), F32),),
+            "svvbb",
+            scratch=landing(2 * steps),
             flops=2 * product_flops,
-            grid=(2 * steps,),
-            blocks={
-                3: pl.BlockSpec(strip, lambda k: (jnp.minimum(k, steps - 1), 0)),
-                4: pl.BlockSpec(strip, lambda k: (jnp.maximum(k - steps, 0), 0)),
-            },
+            room=18,
         )(elements, scaled, local, *matrices)
 
     local = swept(1, local)

time: 120 us -> 124 us (1.033)
  the two profiles are of different devices: /device:TPU:1 before, /device:TPU:2 now
where the time goes in v3:
time: 124 us; the launch traced here: 123 us
  starting transfers between devices  56.2 us (45%)
  waiting for transfers between devices  32.8 us (26%)
  Pallas kernels  31.6 us (25%)
  between operations  1.48 us (1%)
  local copies, waits for them, and re-layouts  1.35 us (1%)
    all_to_all x6, starting transfers between devices, across(): return lax.all_to_all(slots, axis, split_axis=0, concat_axis=0, tiled=True)  37.6 us
    pallas_call x13, Pallas kernels, run(): kernel(*(x if kind == 's' else pltpu.with_memory_space_constraint(x, pltp...  31.6 us
    all_to_all x6, waiting for transfers between devices, across(): return lax.all_to_all(slots, axis, split_axis=0, concat_axis=0, tiled=True)  22.2 us
    ppermute x12, starting transfers between devices, swapped(): lax.ppermute(x, axis, pairs)  18.6 us
    ppermute x12, waiting for transfers between devices, swapped(): lax.ppermute(x, axis, pairs)  10.7 us
  transfers between devices with their start and end apart: 18, of which 9 were waited for; matrix products, arithmetic and copies ran while one was open for 0% of the time, Pallas kernels for 11%

profile of v3, /device:TPU:2, one launch (start us, length us, event | category | flops | bytes accessed | tf_op | source)
XLA Modules:
  0.0 123.5 jit_solution(72986491639294118)
XLA Ops:
  2.4 1.7 %collective-permute-start.2 = (f32[8,256]{1,0:T(8,128)S(1)}, f32[8,256]{1,0:T(8,128)S(1)}, u32[]{:S(2)}, u32[]{:S(2)}) collective-permute-start(f32[8,256]{1,0:T(8,128)S(1)} %get-tuple-element.47), channel_id=1, source_target_pairs={{0,16},{16,0},{32,48},{48,32},{64,80},{80,64},{96,112},{112,96},{1... | collective-permute-start | bytes 24584 | tf_op jit(solution)/shard_map/ppermute | solution.py:350
  4.1 4.0 %collective-permute-start.3 = (f32[8,256]{1,0:T(8,128)S(1)}, f32[8,256]{1,0:T(8,128)S(1)}, u32[]{:S(2)}, u32[]{:S(2)}) collective-permute-start(f32[8,256]{1,0:T(8,128)S(1)} %get-tuple-element.48), channel_id=1, source_target_pairs={{16,32},{32,16},{48,64},{64,48},{80,96},{96,80},{112,128},{128,112... | collective-permute-start | bytes 24584 | tf_op jit(solution)/shard_map/ppermute | solution.py:350
  8.2 3.6 %collective-permute-done.3.g3 = f32[8,256]{1,0:T(8,128)S(1)} collective-permute-done((f32[8,256]{1,0:T(8,128)S(1)}, f32[8,256]{1,0:T(8,128)S(1)}, u32[]{:S(2)}, u32[]{:S(2)}) %collective-permute-start.3) | collective-permute-done | bytes 8224 | tf_op jit(solution)/shard_map/ppermute | solution.py:350
  12.8 10.5 %all-to-all-start = ((f32[16,8,128]{2,1,0:T(8,128)}), f32[16,8,128]{2,1,0:T(8,128)S(1)}, u32[]{:S(2)}, u32[]{:S(2)}) async-start(f32[16,8,128]{2,1,0:T(8,128)} %get-tuple-element.53), calls=%async_computation | async-start | bytes 131072 | tf_op jit(solution)/shard_map/all_to_all | solution.py:356
  23.3 2.5 %first_solve.1.present = f32[8,1024]{1,0:T(8,128)S(1)} custom-call(f32[8,1024]{1,0:T(8,128)S(1)} %get-tuple-element.54.scaled, f32[1024,1024]{1,0:T(8,128)} %bitcast.20), custom_call_target="tpu_custom_call" | custom-call | flops 2147483648 | tf_op jit(solution)/shard_map/first_solve/pallas_call | solution.py:36
  25.9 5.2 %all-to-all-done.got = f32[16,8,128]{2,1,0:T(8,128)S(1)} async-done(((f32[16,8,128]{2,1,0:T(8,128)}), f32[16,8,128]{2,1,0:T(8,128)S(1)}, u32[]{:S(2)}, u32[]{:S(2)}) %all-to-all-start) | async-done | bytes 65568 | tf_op jit(solution)/shard_map/all_to_all | solution.py:356
  32.0 6.5 %all-to-all-start.1 = ((f32[16,8,896]{2,1,0:T(8,128)}), f32[16,8,896]{2,1,0:T(8,128)S(1)}, u32[]{:S(2)}, u32[]{:S(2)}) async-start(f32[16,8,896]{2,1,0:T(8,128)} %pack_picked.1), calls=%async_computation.1 | async-start | bytes 917504 | tf_op jit(solution)/shard_map/all_to_all | solution.py:356
  39.1 3.9 %sweep_once.2.present = f32[8,1024]{1,0:T(8,128)S(1)} custom-call(s32[1,1]{1,0:T(1,128)S(6)} %copy.11.elements, f32[8,1024]{1,0:T(8,128)S(1)} %get-tuple-element.54.scaled, f32[8,1024]{1,0:T(8,128)S(1)} %first_solve.1.present, f32[1024,1024]{1,0:T(8,128)} %bitcast.23, f32[1024,1024]{1,0:T(8,128)} %bitcast.21), custom_call_target="tpu_custom_call" | custom-call | flops 4294967296 | tf_op jit(solution)/shard_map/sweep_once/pallas_call | solution.py:36
  43.0 4.5 %all-to-all-done.1.got.asked = f32[16,8,896]{2,1,0:T(8,128)S(1)} async-done(((f32[16,8,896]{2,1,0:T(8,128)}), f32[16,8,896]{2,1,0:T(8,128)S(1)}, u32[]{:S(2)}, u32[]{:S(2)}) %all-to-all-start.1) | async-done | bytes 458784 | tf_op jit(solution)/shard_map/all_to_all | solution.py:356
  47.5 8.7 %coarse_solve.1 = f32[16,8,128]{2,1,0:T(8,128)} custom-call(f32[16,8,896]{2,1,0:T(8,128)S(1)} %all-to-all-done.1.got.asked, f32[48,12288]{1,0:T(8,128)} %coarse.1), custom_call_target="tpu_custom_call" | custom-call | tf_op jit(solution)/shard_map/coarse_solve/pallas_call | solution.py:36
  56.3 3.5 %all-to-all-start.2 = ((f32[16,8,128]{2,1,0:T(8,128)}), f32[16,8,128]{2,1,0:T(8,128)S(1)}, u32[]{:S(2)}, u32[]{:S(2)}) async-start(f32[16,8,128]{2,1,0:T(8,128)} %coarse_solve.1), calls=%async_computation.2 | async-start | bytes 131072 | tf_op jit(solution)/shard_map/all_to_all | solution.py:356
  59.8 3.9 %sweep_once.3.local = f32[8,1024]{1,0:T(8,128)S(1)} custom-call(s32[1,1]{1,0:T(1,128)S(6)} %copy.11.elements, f32[8,1024]{1,0:T(8,128)S(1)} %get-tuple-element.54.scaled, f32[8,1024]{1,0:T(8,128)S(1)} %sweep_once.2.present, f32[1024,1024]{1,0:T(8,128)} %bitcast.24, f32[1024,1024]{1,0:T(8,128)} %bitcast.22), custom_call_target="tpu_custom_call" | custom-call | flops 4294967296 | tf_op jit(solution)/shard_map/sweep_once/pallas_call | solution.py:36
  63.7 3.9 %all-to-all-done.2.got = f32[16,8,128]{2,1,0:T(8,128)S(1)} async-done(((f32[16,8,128]{2,1,0:T(8,128)}), f32[16,8,128]{2,1,0:T(8,128)S(1)}, u32[]{:S(2)}, u32[]{:S(2)}) %all-to-all-start.2) | async-done | bytes 65568 | tf_op jit(solution)/shard_map/all_to_all | solution.py:356
  68.9 5.7 %all-to-all-start.3 = ((f32[16,8,128]{2,1,0:T(8,128)}), f32[16,8,128]{2,1,0:T(8,128)S(1)}, u32[]{:S(2)}, u32[]{:S(2)}) async-start(f32[16,8,128]{2,1,0:T(8,128)} %pack_solved.1), calls=%async_computation.3 | async-start | bytes 131072 | tf_op jit(solution)/shard_map/all_to_all | solution.py:356
  74.6 2.9 %split_matrix.1 = (bf16[1024,1024]{1,0:T(8,128)(2,1)S(1)}, bf16[1024,1024]{1,0:T(8,128)(2,1)S(1)}) custom-call(f32[1024,1024]{1,0:T(8,128)} %bitcast.25), custom_call_target="tpu_custom_call" | custom-call | flops 2147483648 | tf_op jit(solution)/shard_map/split_matrix/pallas_call | solution.py:36
  78.8 2.0 %all-to-all-done.3.got = f32[16,8,128]{2,1,0:T(8,128)S(1)} async-done(((f32[16,8,128]{2,1,0:T(8,128)}), f32[16,8,128]{2,1,0:T(8,128)S(1)}, u32[]{:S(2)}, u32[]{:S(2)}) %all-to-all-start.3) | async-done | bytes 65568 | tf_op jit(solution)/shard_map/all_to_all | solution.py:356
  82.8 4.4 %collective-permute-start.7 = (f32[8,256]{1,0:T(8,128)S(1)}, f32[8,256]{1,0:T(8,128)S(1)}, u32[]{:S(2)}, u32[]{:S(2)}) collective-permute-start(f32[8,256]{1,0:T(8,128)S(1)} %get-tuple-element.70), channel_id=1, source_target_pairs={{16,32},{32,16},{48,64},{64,48},{80,96},{96,80},{112,128},{128,112... | collective-permute-start | bytes 24584 | tf_op jit(solution)/shard_map/ppermute | solution.py:350
  87.2 3.2 %collective-permute-done.7.g3 = f32[8,256]{1,0:T(8,128)S(1)} collective-permute-done((f32[8,256]{1,0:T(8,128)S(1)}, f32[8,256]{1,0:T(8,128)S(1)}, u32[]{:S(2)}, u32[]{:S(2)}) %collective-permute-start.7) | collective-permute-done | bytes 8224 | tf_op jit(solution)/shard_map/ppermute | solution.py:350
  90.4 3.2 %apply_operator.1 = (f32[8,1024]{1,0:T(8,128)S(1)}, f32[8,1024]{1,0:T(8,128)S(1)}, f32[8,256]{1,0:T(8,128)S(1)}, f32[8,256]{1,0:T(8,128)S(1)}, f32[8,256]{1,0:T(...) custom-call(f32[8,1024]{1,0:T(8,128)S(1)} %get-tuple-element.66.t, f32[8,256]{1,0:T(8,128)S(1)} %collective-permute-done.4.g0, ...), custom_call_target="tpu_custom_call" | custom-call | tf_op jit(solution)/shard_map/apply_operator/pallas_call | solution.py:36
  93.6 6.3 %all-to-all-start.4 = ((f32[16,8,128]{2,1,0:T(8,128)}), f32[16,8,128]{2,1,0:T(8,128)S(1)}, u32[]{:S(2)}, u32[]{:S(2)}) async-start(f32[16,8,128]{2,1,0:T(8,128)} %get-tuple-element.74), calls=%async_computation.4 | async-start | bytes 131072 | tf_op jit(solution)/shard_map/all_to_all | solution.py:356
  101.1 6.5 %all-to-all-done.4.got = f32[16,8,128]{2,1,0:T(8,128)S(1)} async-done(((f32[16,8,128]{2,1,0:T(8,128)}), f32[16,8,128]{2,1,0:T(8,128)S(1)}, u32[]{:S(2)}, u32[]{:S(2)}) %all-to-all-start.4) | async-done | bytes 65568 | tf_op jit(solution)/shard_map/all_to_all | solution.py:356
  108.3 5.2 %all-to-all-start.5 = ((f32[16,8,128]{2,1,0:T(8,128)}), f32[16,8,128]{2,1,0:T(8,128)S(1)}, u32[]{:S(2)}, u32[]{:S(2)}) async-start(f32[16,8,128]{2,1,0:T(8,128)} %subtotal.1), calls=%async_computation.5 | async-start | bytes 131072 | tf_op jit(solution)/shard_map/all_to_all | solution.py:356
  115.0 4.0 %collective-permute-start.11 = (f32[8,256]{1,0:T(8,128)S(1)}, f32[8,256]{1,0:T(8,128)S(1)}, u32[]{:S(2)}, u32[]{:S(2)}) collective-permute-start(f32[8,256]{1,0:T(8,128)S(1)} %get-tuple-element.81), channel_id=1, source_target_pairs={{16,32},{32,16},{48,64},{64,48},{80,96},{96,80},{112,128},{128,112... | collective-permute-start | bytes 24584 | tf_op jit(solution)/shard_map/ppermute | solution.py:350
  118.9 3.7 %collective-permute-done.11.g3 = f32[8,256]{1,0:T(8,128)S(1)} collective-permute-done((f32[8,256]{1,0:T(8,128)S(1)}, f32[8,256]{1,0:T(8,128)S(1)}, u32[]{:S(2)}, u32[]{:S(2)}) %collective-permute-start.11) | collective-permute-done | bytes 8224 | tf_op jit(solution)/shard_map/ppermute | solution.py:350
  (27 shorter events, 12.6 us)
Async XLA Ops:
  1.8 6.4 %collective-permute-start = (f32[8,256]{1,0:T(8,128)S(1)}, f32[8,256]{1,0:T(8,128)S(1)}, u32[]{:S(2)}, u32[]{:S(2)}) collective-permute-start(f32[8,256]{1,0:T(8,128)S(1)} %get-tuple-element.45), channel_id=1, source_target_pairs={{0,1},{1,0},{2,3},{3,2},{4,5},{5,4},{6,7},{7,6},{8,9},{9,8},{10,11... | collective-permute-start | bytes 24584 | tf_op jit(solution)/shard_map/ppermute | solution.py:350
  1.8 6.4 %collective-permute-start.1 = (f32[8,256]{1,0:T(8,128)S(1)}, f32[8,256]{1,0:T(8,128)S(1)}, u32[]{:S(2)}, u32[]{:S(2)}) collective-permute-start(f32[8,256]{1,0:T(8,128)S(1)} %get-tuple-element.46), channel_id=1, source_target_pairs={{1,2},{2,1},{3,4},{4,3},{5,6},{6,5},{7,8},{8,7},{9,10},{10,9},{11,... | collective-permute-start | bytes 24584 | tf_op jit(solution)/shard_map/ppermute | solution.py:350
  2.4 5.7 %collective-permute-start.2 = (f32[8,256]{1,0:T(8,128)S(1)}, f32[8,256]{1,0:T(8,128)S(1)}, u32[]{:S(2)}, u32[]{:S(2)}) collective-permute-start(f32[8,256]{1,0:T(8,128)S(1)} %get-tuple-element.47), channel_id=1, source_target_pairs={{0,16},{16,0},{32,48},{48,32},{64,80},{80,64},{96,112},{112,96},{1... | collective-permute-start | bytes 24584 | tf_op jit(solution)/shard_map/ppermute | solution.py:350
  4.1 7.6 %collective-permute-start.3 = (f32[8,256]{1,0:T(8,128)S(1)}, f32[8,256]{1,0:T(8,128)S(1)}, u32[]{:S(2)}, u32[]{:S(2)}) collective-permute-start(f32[8,256]{1,0:T(8,128)S(1)} %get-tuple-element.48), channel_id=1, source_target_pairs={{16,32},{32,16},{48,64},{64,48},{80,96},{96,80},{112,128},{128,112... | collective-permute-start | bytes 24584 | tf_op jit(solution)/shard_map/ppermute | solution.py:350
  12.8 18.3 %all-to-all-start = ((f32[16,8,128]{2,1,0:T(8,128)}), f32[16,8,128]{2,1,0:T(8,128)S(1)}, u32[]{:S(2)}, u32[]{:S(2)}) async-start(f32[16,8,128]{2,1,0:T(8,128)} %get-tuple-element.53), calls=%async_computation | async-start | bytes 131072 | tf_op jit(solution)/shard_map/all_to_all | solution.py:356
  32.0 15.5 %all-to-all-start.1 = ((f32[16,8,896]{2,1,0:T(8,128)}), f32[16,8,896]{2,1,0:T(8,128)S(1)}, u32[]{:S(2)}, u32[]{:S(2)}) async-start(f32[16,8,896]{2,1,0:T(8,128)} %pack_picked.1), calls=%async_computation.1 | async-start | bytes 917504 | tf_op jit(solution)/shard_map/all_to_all | solution.py:356
  56.3 11.3 %all-to-all-start.2 = ((f32[16,8,128]{2,1,0:T(8,128)}), f32[16,8,128]{2,1,0:T(8,128)S(1)}, u32[]{:S(2)}, u32[]{:S(2)}) async-start(f32[16,8,128]{2,1,0:T(8,128)} %coarse_solve.1), calls=%async_computation.2 | async-start | bytes 131072 | tf_op jit(solution)/shard_map/all_to_all | solution.py:356
  68.9 12.0 %all-to-all-start.3 = ((f32[16,8,128]{2,1,0:T(8,128)}), f32[16,8,128]{2,1,0:T(8,128)S(1)}, u32[]{:S(2)}, u32[]{:S(2)}) async-start(f32[16,8,128]{2,1,0:T(8,128)} %pack_solved.1), calls=%async_computation.3 | async-start | bytes 131072 | tf_op jit(solution)/shard_map/all_to_all | solution.py:356
  77.5 1.4 %copy-start = (bf16[1024,1024]{1,0:T(8,128)(2,1)}, bf16[1024,1024]{1,0:T(8,128)(2,1)S(1)}, u32[]{:S(2)}) copy-start(bf16[1024,1024]{1,0:T(8,128)(2,1)S(1)} %get-tuple-element.72.low) | copy-start | bytes 6291460
  81.4 5.8 %collective-permute-start.4 = (f32[8,256]{1,0:T(8,128)S(1)}, f32[8,256]{1,0:T(8,128)S(1)}, u32[]{:S(2)}, u32[]{:S(2)}) collective-permute-start(f32[8,256]{1,0:T(8,128)S(1)} %get-tuple-element.67), channel_id=1, source_target_pairs={{0,1},{1,0},{2,3},{3,2},{4,5},{5,4},{6,7},{7,6},{8,9},{9,8},{10,11... | collective-permute-start | bytes 24584 | tf_op jit(solution)/shard_map/ppermute | solution.py:350
  81.4 5.8 %collective-permute-start.5 = (f32[8,256]{1,0:T(8,128)S(1)}, f32[8,256]{1,0:T(8,128)S(1)}, u32[]{:S(2)}, u32[]{:S(2)}) collective-permute-start(f32[8,256]{1,0:T(8,128)S(1)} %get-tuple-element.68), channel_id=1, source_target_pairs={{1,2},{2,1},{3,4},{4,3},{5,6},{6,5},{7,8},{8,7},{9,10},{10,9},{11,... | collective-permute-start | bytes 24584 | tf_op jit(solution)/shard_map/ppermute | solution.py:350
  82.1 5.1 %collective-permute-start.6 = (f32[8,256]{1,0:T(8,128)S(1)}, f32[8,256]{1,0:T(8,128)S(1)}, u32[]{:S(2)}, u32[]{:S(2)}) collective-permute-start(f32[8,256]{1,0:T(8,128)S(1)} %get-tuple-element.69), channel_id=1, source_target_pairs={{0,16},{16,0},{32,48},{48,32},{64,80},{80,64},{96,112},{112,96},{1... | collective-permute-start | bytes 24584 | tf_op jit(solution)/shard_map/ppermute | solution.py:350
  82.8 7.6 %collective-permute-start.7 = (f32[8,256]{1,0:T(8,128)S(1)}, f32[8,256]{1,0:T(8,128)S(1)}, u32[]{:S(2)}, u32[]{:S(2)}) collective-permute-start(f32[8,256]{1,0:T(8,128)S(1)} %get-tuple-element.70), channel_id=1, source_target_pairs={{16,32},{32,16},{48,64},{64,48},{80,96},{96,80},{112,128},{128,112... | collective-permute-start | bytes 24584 | tf_op jit(solution)/shard_map/ppermute | solution.py:350
  93.6 14.1 %all-to-all-start.4 = ((f32[16,8,128]{2,1,0:T(8,128)}), f32[16,8,128]{2,1,0:T(8,128)S(1)}, u32[]{:S(2)}, u32[]{:S(2)}) async-start(f32[16,8,128]{2,1,0:T(8,128)} %get-tuple-element.74), calls=%async_computation.4 | async-start | bytes 131072 | tf_op jit(solution)/shard_map/all_to_all | solution.py:356
  99.9 1.3 %collective-permute-start.8 = (f32[8,256]{1,0:T(8,128)S(1)}, f32[8,256]{1,0:T(8,128)S(1)}, u32[]{:S(2)}, u32[]{:S(2)}) collective-permute-start(f32[8,256]{1,0:T(8,128)S(1)} %get-tuple-element.75), channel_id=1, source_target_pairs={{0,1},{1,0},{2,3},{3,2},{4,5},{5,4},{6,7},{7,6},{8,9},{9,8},{10,11... | collective-permute-start | bytes 24584 | tf_op jit(solution)/shard_map/ppermute | solution.py:350
  100.3 0.9 collective-permute-start.9
  108.3 14.3 %all-to-all-start.5 = ((f32[16,8,128]{2,1,0:T(8,128)}), f32[16,8,128]{2,1,0:T(8,128)S(1)}, u32[]{:S(2)}, u32[]{:S(2)}) async-start(f32[16,8,128]{2,1,0:T(8,128)} %subtotal.1), calls=%async_computation.5 | async-start | bytes 131072 | tf_op jit(solution)/shard_map/all_to_all | solution.py:356
  113.5 5.4 %collective-permute-start.10 = (f32[8,256]{1,0:T(8,128)S(1)}, f32[8,256]{1,0:T(8,128)S(1)}, u32[]{:S(2)}, u32[]{:S(2)}) collective-permute-start(f32[8,256]{1,0:T(8,128)S(1)} %get-tuple-element.80), channel_id=1, source_target_pairs={{0,16},{16,0},{32,48},{48,32},{64,80},{80,64},{96,112},{112,96},{1... | collective-permute-start | bytes 24584 | tf_op jit(solution)/shard_map/ppermute | solution.py:350
  115.0 7.6 %collective-permute-start.11 = (f32[8,256]{1,0:T(8,128)S(1)}, f32[8,256]{1,0:T(8,128)S(1)}, u32[]{:S(2)}, u32[]{:S(2)}) collective-permute-start(f32[8,256]{1,0:T(8,128)S(1)} %get-tuple-element.81), channel_id=1, source_target_pairs={{16,32},{32,16},{48,64},{64,48},{80,96},{96,80},{112,128},{128,112... | collective-permute-start | bytes 24584 | tf_op jit(solution)/shard_map/ppermute | solution.py:350

commit v4 on v3

--- a/solution.py
+++ b/solution.py
@@ -345,7 +345,7 @@
 
 def swapped(sends):
     even = [(i, i ^ 1) for i in range(SIDE)]
-    odd = [(i, ((i + 1) ^ 1) - 1) for i in range(1, SIDE - 1)]
+    odd = [(i, ((i + 1) ^ 1) - 1) for i in range(1, SIDE - 1)] + [(0, SIDE - 1), (SIDE - 1, 0)]
     return [
         lax.ppermute(x, axis, pairs)
         for x, axis, pairs in zip(sends, (COL, COL, ROW, ROW), (even, odd, even, odd))

time: 124 us -> 118 us (0.952)
  the two profiles are of different devices: /device:TPU:2 before, /device:TPU:1 now
where the time goes in v4:
time: 118 us; the launch traced here: 117 us
  starting transfers between devices  52.2 us (44%)
  Pallas kernels  31.6 us (27%)
  waiting for transfers between devices  30.5 us (26%)
  between operations  1.38 us (1%)
  local copies, waits for them, and re-layouts  1.35 us (1%)
    all_to_all x6, starting transfers between devices, across(): return lax.all_to_all(slots, axis, split_axis=0, concat_axis=0, tiled=True)  32.8 us
    pallas_call x13, Pallas kernels, run(): kernel(*(x if kind == 's' else pltpu.with_memory_space_constraint(x, pltp...  31.6 us
    all_to_all x6, waiting for transfers between devices, across(): return lax.all_to_all(slots, axis, split_axis=0, concat_axis=0, tiled=True)  20.5 us
    ppermute x12, starting transfers between devices, swapped(): lax.ppermute(x, axis, pairs)  19.4 us
    ppermute x12, waiting for transfers between devices, swapped(): lax.ppermute(x, axis, pairs)  10.1 us
  transfers between devices with their start and end apart: 18, of which 10 were waited for; matrix products, arithmetic and copies ran while one was open for 0% of the time, Pallas kernels for 11%

profile of v4, /device:TPU:1, one launch (start us, length us, event | category | flops | bytes accessed | tf_op | source)
XLA Modules:
  0.0 117.0 jit_solution(12776794208743152206)
XLA Ops:
  1.8 3.2 %collective-permute-start = (f32[8,256]{1,0:T(8,128)S(1)}, f32[8,256]{1,0:T(8,128)S(1)}, u32[]{:S(2)}, u32[]{:S(2)}) collective-permute-start(f32[8,256]{1,0:T(8,128)S(1)} %get-tuple-element.45), channel_id=1, source_target_pairs={{0,1},{1,0},{2,3},{3,2},{4,5},{5,4},{6,7},{7,6},{8,9},{9,8},{10,11... | collective-permute-start | bytes 24584 | tf_op jit(solution)/shard_map/ppermute | solution.py:350
  6.2 4.1 %collective-permute-start.3 = (f32[8,256]{1,0:T(8,128)S(1)}, f32[8,256]{1,0:T(8,128)S(1)}, u32[]{:S(2)}, u32[]{:S(2)}) collective-permute-start(f32[8,256]{1,0:T(8,128)S(1)} %get-tuple-element.48), channel_id=1, source_target_pairs={{16,32},{32,16},{48,64},{64,48},{80,96},{96,80},{112,128},{128,112... | collective-permute-start | bytes 24584 | tf_op jit(solution)/shard_map/ppermute | solution.py:350
  13.1 9.1 %all-to-all-start = ((f32[16,8,128]{2,1,0:T(8,128)}), f32[16,8,128]{2,1,0:T(8,128)S(1)}, u32[]{:S(2)}, u32[]{:S(2)}) async-start(f32[16,8,128]{2,1,0:T(8,128)} %get-tuple-element.53), calls=%async_computation | async-start | bytes 131072 | tf_op jit(solution)/shard_map/all_to_all | solution.py:356
  22.1 2.5 %first_solve.1.present = f32[8,1024]{1,0:T(8,128)S(1)} custom-call(f32[8,1024]{1,0:T(8,128)S(1)} %get-tuple-element.54.scaled, f32[1024,1024]{1,0:T(8,128)} %bitcast.20), custom_call_target="tpu_custom_call" | custom-call | flops 2147483648 | tf_op jit(solution)/shard_map/first_solve/pallas_call | solution.py:36
  24.7 5.3 %all-to-all-done.got = f32[16,8,128]{2,1,0:T(8,128)S(1)} async-done(((f32[16,8,128]{2,1,0:T(8,128)}), f32[16,8,128]{2,1,0:T(8,128)S(1)}, u32[]{:S(2)}, u32[]{:S(2)}) %all-to-all-start) | async-done | bytes 65568 | tf_op jit(solution)/shard_map/all_to_all | solution.py:356
  30.9 5.5 %all-to-all-start.1 = ((f32[16,8,896]{2,1,0:T(8,128)}), f32[16,8,896]{2,1,0:T(8,128)S(1)}, u32[]{:S(2)}, u32[]{:S(2)}) async-start(f32[16,8,896]{2,1,0:T(8,128)} %pack_picked.1), calls=%async_computation.1 | async-start | bytes 917504 | tf_op jit(solution)/shard_map/all_to_all | solution.py:356
  37.0 3.9 %sweep_once.2.present = f32[8,1024]{1,0:T(8,128)S(1)} custom-call(s32[1,1]{1,0:T(1,128)S(6)} %copy.11.elements, f32[8,1024]{1,0:T(8,128)S(1)} %get-tuple-element.54.scaled, f32[8,1024]{1,0:T(8,128)S(1)} %first_solve.1.present, f32[1024,1024]{1,0:T(8,128)} %bitcast.23, f32[1024,1024]{1,0:T(8,128)} %bitcast.21), custom_call_target="tpu_custom_call" | custom-call | flops 4294967296 | tf_op jit(solution)/shard_map/sweep_once/pallas_call | solution.py:36
  40.9 5.2 %all-to-all-done.1.got.asked = f32[16,8,896]{2,1,0:T(8,128)S(1)} async-done(((f32[16,8,896]{2,1,0:T(8,128)}), f32[16,8,896]{2,1,0:T(8,128)S(1)}, u32[]{:S(2)}, u32[]{:S(2)}) %all-to-all-start.1) | async-done | bytes 458784 | tf_op jit(solution)/shard_map/all_to_all | solution.py:356
  46.1 8.7 %coarse_solve.1 = f32[16,8,128]{2,1,0:T(8,128)} custom-call(f32[16,8,896]{2,1,0:T(8,128)S(1)} %all-to-all-done.1.got.asked, f32[48,12288]{1,0:T(8,128)} %coarse.1), custom_call_target="tpu_custom_call" | custom-call | tf_op jit(solution)/shard_map/coarse_solve/pallas_call | solution.py:36
  54.8 5.3 %all-to-all-start.2 = ((f32[16,8,128]{2,1,0:T(8,128)}), f32[16,8,128]{2,1,0:T(8,128)S(1)}, u32[]{:S(2)}, u32[]{:S(2)}) async-start(f32[16,8,128]{2,1,0:T(8,128)} %coarse_solve.1), calls=%async_computation.2 | async-start | bytes 131072 | tf_op jit(solution)/shard_map/all_to_all | solution.py:356
  60.1 3.9 %sweep_once.3.local = f32[8,1024]{1,0:T(8,128)S(1)} custom-call(s32[1,1]{1,0:T(1,128)S(6)} %copy.11.elements, f32[8,1024]{1,0:T(8,128)S(1)} %get-tuple-element.54.scaled, f32[8,1024]{1,0:T(8,128)S(1)} %sweep_once.2.present, f32[1024,1024]{1,0:T(8,128)} %bitcast.24, f32[1024,1024]{1,0:T(8,128)} %bitcast.22), custom_call_target="tpu_custom_call" | custom-call | flops 4294967296 | tf_op jit(solution)/shard_map/sweep_once/pallas_call | solution.py:36
  64.0 3.9 %all-to-all-done.2.got = f32[16,8,128]{2,1,0:T(8,128)S(1)} async-done(((f32[16,8,128]{2,1,0:T(8,128)}), f32[16,8,128]{2,1,0:T(8,128)S(1)}, u32[]{:S(2)}, u32[]{:S(2)}) %all-to-all-start.2) | async-done | bytes 65568 | tf_op jit(solution)/shard_map/all_to_all | solution.py:356
  69.2 3.5 %all-to-all-start.3 = ((f32[16,8,128]{2,1,0:T(8,128)}), f32[16,8,128]{2,1,0:T(8,128)S(1)}, u32[]{:S(2)}, u32[]{:S(2)}) async-start(f32[16,8,128]{2,1,0:T(8,128)} %pack_solved.1), calls=%async_computation.3 | async-start | bytes 131072 | tf_op jit(solution)/shard_map/all_to_all | solution.py:356
  72.7 2.9 %split_matrix.1 = (bf16[1024,1024]{1,0:T(8,128)(2,1)S(1)}, bf16[1024,1024]{1,0:T(8,128)(2,1)S(1)}) custom-call(f32[1024,1024]{1,0:T(8,128)} %bitcast.25), custom_call_target="tpu_custom_call" | custom-call | flops 2147483648 | tf_op jit(solution)/shard_map/split_matrix/pallas_call | solution.py:36
  77.0 2.2 %all-to-all-done.3.got = f32[16,8,128]{2,1,0:T(8,128)S(1)} async-done(((f32[16,8,128]{2,1,0:T(8,128)}), f32[16,8,128]{2,1,0:T(8,128)S(1)}, u32[]{:S(2)}, u32[]{:S(2)}) %all-to-all-start.3) | async-done | bytes 65568 | tf_op jit(solution)/shard_map/all_to_all | solution.py:356
  81.9 1.9 %collective-permute-start.7 = (f32[8,256]{1,0:T(8,128)S(1)}, f32[8,256]{1,0:T(8,128)S(1)}, u32[]{:S(2)}, u32[]{:S(2)}) collective-permute-start(f32[8,256]{1,0:T(8,128)S(1)} %get-tuple-element.70), channel_id=1, source_target_pairs={{16,32},{32,16},{48,64},{64,48},{80,96},{96,80},{112,128},{128,112... | collective-permute-start | bytes 24584 | tf_op jit(solution)/shard_map/ppermute | solution.py:350
  84.2 3.5 %collective-permute-done.7.g3 = f32[8,256]{1,0:T(8,128)S(1)} collective-permute-done((f32[8,256]{1,0:T(8,128)S(1)}, f32[8,256]{1,0:T(8,128)S(1)}, u32[]{:S(2)}, u32[]{:S(2)}) %collective-permute-start.7) | collective-permute-done | bytes 8224 | tf_op jit(solution)/shard_map/ppermute | solution.py:350
  87.7 3.2 %apply_operator.1 = (f32[8,1024]{1,0:T(8,128)S(1)}, f32[8,1024]{1,0:T(8,128)S(1)}, f32[8,256]{1,0:T(8,128)S(1)}, f32[8,256]{1,0:T(8,128)S(1)}, f32[8,256]{1,0:T(...) custom-call(f32[8,1024]{1,0:T(8,128)S(1)} %get-tuple-element.66.t, f32[8,256]{1,0:T(8,128)S(1)} %collective-permute-done.4.g0, ...), custom_call_target="tpu_custom_call" | custom-call | tf_op jit(solution)/shard_map/apply_operator/pallas_call | solution.py:36
  90.9 5.9 %all-to-all-start.4 = ((f32[16,8,128]{2,1,0:T(8,128)}), f32[16,8,128]{2,1,0:T(8,128)S(1)}, u32[]{:S(2)}, u32[]{:S(2)}) async-start(f32[16,8,128]{2,1,0:T(8,128)} %get-tuple-element.74), calls=%async_computation.4 | async-start | bytes 131072 | tf_op jit(solution)/shard_map/all_to_all | solution.py:356
  98.5 2.2 %collective-permute-done.9.g1 = f32[8,256]{1,0:T(8,128)S(1)} collective-permute-done((f32[8,256]{1,0:T(8,128)S(1)}, f32[8,256]{1,0:T(8,128)S(1)}, u32[]{:S(2)}, u32[]{:S(2)}) %collective-permute-start.9) | collective-permute-done | bytes 8224 | tf_op jit(solution)/shard_map/ppermute | solution.py:350
  100.7 3.9 %all-to-all-done.4.got = f32[16,8,128]{2,1,0:T(8,128)S(1)} async-done(((f32[16,8,128]{2,1,0:T(8,128)}), f32[16,8,128]{2,1,0:T(8,128)S(1)}, u32[]{:S(2)}, u32[]{:S(2)}) %all-to-all-start.4) | async-done | bytes 65568 | tf_op jit(solution)/shard_map/all_to_all | solution.py:356
  105.3 3.5 %all-to-all-start.5 = ((f32[16,8,128]{2,1,0:T(8,128)}), f32[16,8,128]{2,1,0:T(8,128)S(1)}, u32[]{:S(2)}, u32[]{:S(2)}) async-start(f32[16,8,128]{2,1,0:T(8,128)} %subtotal.1), calls=%async_computation.5 | async-start | bytes 131072 | tf_op jit(solution)/shard_map/all_to_all | solution.py:356
  110.0 4.0 %collective-permute-start.11 = (f32[8,256]{1,0:T(8,128)S(1)}, f32[8,256]{1,0:T(8,128)S(1)}, u32[]{:S(2)}, u32[]{:S(2)}) collective-permute-start(f32[8,256]{1,0:T(8,128)S(1)} %get-tuple-element.81), channel_id=1, source_target_pairs={{16,32},{32,16},{48,64},{64,48},{80,96},{96,80},{112,128},{128,112... | collective-permute-start | bytes 24584 | tf_op jit(solution)/shard_map/ppermute | solution.py:350
  114.0 2.1 %collective-permute-done.11.g3 = f32[8,256]{1,0:T(8,128)S(1)} collective-permute-done((f32[8,256]{1,0:T(8,128)S(1)}, f32[8,256]{1,0:T(8,128)S(1)}, u32[]{:S(2)}, u32[]{:S(2)}) %collective-permute-start.11) | collective-permute-done | bytes 8224 | tf_op jit(solution)/shard_map/ppermute | solution.py:350
  (27 shorter events, 16.3 us)
Async XLA Ops:
  1.8 8.5 %collective-permute-start = (f32[8,256]{1,0:T(8,128)S(1)}, f32[8,256]{1,0:T(8,128)S(1)}, u32[]{:S(2)}, u32[]{:S(2)}) collective-permute-start(f32[8,256]{1,0:T(8,128)S(1)} %get-tuple-element.45), channel_id=1, source_target_pairs={{0,1},{1,0},{2,3},{3,2},{4,5},{5,4},{6,7},{7,6},{8,9},{9,8},{10,11... | collective-permute-start | bytes 24584 | tf_op jit(solution)/shard_map/ppermute | solution.py:350
  5.0 5.3 %collective-permute-start.1 = (f32[8,256]{1,0:T(8,128)S(1)}, f32[8,256]{1,0:T(8,128)S(1)}, u32[]{:S(2)}, u32[]{:S(2)}) collective-permute-start(f32[8,256]{1,0:T(8,128)S(1)} %get-tuple-element.46), channel_id=1, source_target_pairs={{1,2},{2,1},{3,4},{4,3},{5,6},{6,5},{7,8},{8,7},{9,10},{10,9},{11,... | collective-permute-start | bytes 24584 | tf_op jit(solution)/shard_map/ppermute | solution.py:350
  5.0 5.3 %collective-permute-start.2 = (f32[8,256]{1,0:T(8,128)S(1)}, f32[8,256]{1,0:T(8,128)S(1)}, u32[]{:S(2)}, u32[]{:S(2)}) collective-permute-start(f32[8,256]{1,0:T(8,128)S(1)} %get-tuple-element.47), channel_id=1, source_target_pairs={{0,16},{16,0},{32,48},{48,32},{64,80},{80,64},{96,112},{112,96},{1... | collective-permute-start | bytes 24584 | tf_op jit(solution)/shard_map/ppermute | solution.py:350
  6.2 5.8 %collective-permute-start.3 = (f32[8,256]{1,0:T(8,128)S(1)}, f32[8,256]{1,0:T(8,128)S(1)}, u32[]{:S(2)}, u32[]{:S(2)}) collective-permute-start(f32[8,256]{1,0:T(8,128)S(1)} %get-tuple-element.48), channel_id=1, source_target_pairs={{16,32},{32,16},{48,64},{64,48},{80,96},{96,80},{112,128},{128,112... | collective-permute-start | bytes 24584 | tf_op jit(solution)/shard_map/ppermute | solution.py:350
  13.1 16.9 %all-to-all-start = ((f32[16,8,128]{2,1,0:T(8,128)}), f32[16,8,128]{2,1,0:T(8,128)S(1)}, u32[]{:S(2)}, u32[]{:S(2)}) async-start(f32[16,8,128]{2,1,0:T(8,128)} %get-tuple-element.53), calls=%async_computation | async-start | bytes 131072 | tf_op jit(solution)/shard_map/all_to_all | solution.py:356
  30.9 15.2 %all-to-all-start.1 = ((f32[16,8,896]{2,1,0:T(8,128)}), f32[16,8,896]{2,1,0:T(8,128)S(1)}, u32[]{:S(2)}, u32[]{:S(2)}) async-start(f32[16,8,896]{2,1,0:T(8,128)} %pack_picked.1), calls=%async_computation.1 | async-start | bytes 917504 | tf_op jit(solution)/shard_map/all_to_all | solution.py:356
  54.8 13.1 %all-to-all-start.2 = ((f32[16,8,128]{2,1,0:T(8,128)}), f32[16,8,128]{2,1,0:T(8,128)S(1)}, u32[]{:S(2)}, u32[]{:S(2)}) async-start(f32[16,8,128]{2,1,0:T(8,128)} %coarse_solve.1), calls=%async_computation.2 | async-start | bytes 131072 | tf_op jit(solution)/shard_map/all_to_all | solution.py:356
  69.2 10.0 %all-to-all-start.3 = ((f32[16,8,128]{2,1,0:T(8,128)}), f32[16,8,128]{2,1,0:T(8,128)S(1)}, u32[]{:S(2)}, u32[]{:S(2)}) async-start(f32[16,8,128]{2,1,0:T(8,128)} %pack_solved.1), calls=%async_computation.3 | async-start | bytes 131072 | tf_op jit(solution)/shard_map/all_to_all | solution.py:356
  75.6 1.4 %copy-start = (bf16[1024,1024]{1,0:T(8,128)(2,1)}, bf16[1024,1024]{1,0:T(8,128)(2,1)S(1)}, u32[]{:S(2)}) copy-start(bf16[1024,1024]{1,0:T(8,128)(2,1)S(1)} %get-tuple-element.72.low) | copy-start | bytes 6291460
  79.8 4.0 %collective-permute-start.4 = (f32[8,256]{1,0:T(8,128)S(1)}, f32[8,256]{1,0:T(8,128)S(1)}, u32[]{:S(2)}, u32[]{:S(2)}) collective-permute-start(f32[8,256]{1,0:T(8,128)S(1)} %get-tuple-element.67), channel_id=1, source_target_pairs={{0,1},{1,0},{2,3},{3,2},{4,5},{5,4},{6,7},{7,6},{8,9},{9,8},{10,11... | collective-permute-start | bytes 24584 | tf_op jit(solution)/shard_map/ppermute | solution.py:350
  81.1 3.1 %collective-permute-start.5 = (f32[8,256]{1,0:T(8,128)S(1)}, f32[8,256]{1,0:T(8,128)S(1)}, u32[]{:S(2)}, u32[]{:S(2)}) collective-permute-start(f32[8,256]{1,0:T(8,128)S(1)} %get-tuple-element.68), channel_id=1, source_target_pairs={{1,2},{2,1},{3,4},{4,3},{5,6},{6,5},{7,8},{8,7},{9,10},{10,9},{11,... | collective-permute-start | bytes 24584 | tf_op jit(solution)/shard_map/ppermute | solution.py:350
  81.6 2.6 %collective-permute-start.6 = (f32[8,256]{1,0:T(8,128)S(1)}, f32[8,256]{1,0:T(8,128)S(1)}, u32[]{:S(2)}, u32[]{:S(2)}) collective-permute-start(f32[8,256]{1,0:T(8,128)S(1)} %get-tuple-element.69), channel_id=1, source_target_pairs={{0,16},{16,0},{32,48},{48,32},{64,80},{80,64},{96,112},{112,96},{1... | collective-permute-start | bytes 24584 | tf_op jit(solution)/shard_map/ppermute | solution.py:350
  81.9 5.8 %collective-permute-start.7 = (f32[8,256]{1,0:T(8,128)S(1)}, f32[8,256]{1,0:T(8,128)S(1)}, u32[]{:S(2)}, u32[]{:S(2)}) collective-permute-start(f32[8,256]{1,0:T(8,128)S(1)} %get-tuple-element.70), channel_id=1, source_target_pairs={{16,32},{32,16},{48,64},{64,48},{80,96},{96,80},{112,128},{128,112... | collective-permute-start | bytes 24584 | tf_op jit(solution)/shard_map/ppermute | solution.py:350
  90.9 13.8 %all-to-all-start.4 = ((f32[16,8,128]{2,1,0:T(8,128)}), f32[16,8,128]{2,1,0:T(8,128)S(1)}, u32[]{:S(2)}, u32[]{:S(2)}) async-start(f32[16,8,128]{2,1,0:T(8,128)} %get-tuple-element.74), calls=%async_computation.4 | async-start | bytes 131072 | tf_op jit(solution)/shard_map/all_to_all | solution.py:356
  96.8 1.8 %collective-permute-start.8 = (f32[8,256]{1,0:T(8,128)S(1)}, f32[8,256]{1,0:T(8,128)S(1)}, u32[]{:S(2)}, u32[]{:S(2)}) collective-permute-start(f32[8,256]{1,0:T(8,128)S(1)} %get-tuple-element.75), channel_id=1, source_target_pairs={{0,1},{1,0},{2,3},{3,2},{4,5},{5,4},{6,7},{7,6},{8,9},{9,8},{10,11... | collective-permute-start | bytes 24584 | tf_op jit(solution)/shard_map/ppermute | solution.py:350
  96.9 3.8 %collective-permute-start.9 = (f32[8,256]{1,0:T(8,128)S(1)}, f32[8,256]{1,0:T(8,128)S(1)}, u32[]{:S(2)}, u32[]{:S(2)}) collective-permute-start(f32[8,256]{1,0:T(8,128)S(1)} %get-tuple-element.76), channel_id=1, source_target_pairs={{1,2},{2,1},{3,4},{4,3},{5,6},{6,5},{7,8},{8,7},{9,10},{10,9},{11,... | collective-permute-start | bytes 24584 | tf_op jit(solution)/shard_map/ppermute | solution.py:350
  105.3 10.9 %all-to-all-start.5 = ((f32[16,8,128]{2,1,0:T(8,128)}), f32[16,8,128]{2,1,0:T(8,128)S(1)}, u32[]{:S(2)}, u32[]{:S(2)}) async-start(f32[16,8,128]{2,1,0:T(8,128)} %subtotal.1), calls=%async_computation.5 | async-start | bytes 131072 | tf_op jit(solution)/shard_map/all_to_all | solution.py:356
  108.8 5.2 %collective-permute-start.10 = (f32[8,256]{1,0:T(8,128)S(1)}, f32[8,256]{1,0:T(8,128)S(1)}, u32[]{:S(2)}, u32[]{:S(2)}) collective-permute-start(f32[8,256]{1,0:T(8,128)S(1)} %get-tuple-element.80), channel_id=1, source_target_pairs={{0,16},{16,0},{32,48},{48,32},{64,80},{80,64},{96,112},{112,96},{1... | collective-permute-start | bytes 24584 | tf_op jit(solution)/shard_map/ppermute | solution.py:350
  110.0 6.1 %collective-permute-start.11 = (f32[8,256]{1,0:T(8,128)S(1)}, f32[8,256]{1,0:T(8,128)S(1)}, u32[]{:S(2)}, u32[]{:S(2)}) collective-permute-start(f32[8,256]{1,0:T(8,128)S(1)} %get-tuple-element.81), channel_id=1, source_target_pairs={{16,32},{32,16},{48,64},{64,48},{80,96},{96,80},{112,128},{128,112... | collective-permute-start | bytes 24584 | tf_op jit(solution)/shard_map/ppermute | solution.py:350

commit v5 on v4

--- a/solution.py
+++ b/solution.py
@@ -451,7 +451,7 @@
     sends, slots = rest[:4], rest[4]
     got = swapped(sends)
     gathered = across(slots, COL)
-    gathered, got[0], got[1] = lax.optimization_barrier((gathered, got[0], got[1]))
+    gathered, got[2], got[3] = lax.optimization_barrier((gathered, got[2], got[3]))
     slots = call(subtotal, tiles, "v")(gathered)
     gathered = across(slots, ROW)
     whole = jax.ShapeDtypeStruct((8, unknowns), F32)

time: 118 us -> 117 us (level)
  starting transfers between devices: 52.2 us -> 48.3 us
  waiting for transfers between devices: 30.5 us -> 33.4 us
    ppermute x12, starting transfers between devices: 19.4 us -> 15.5 us  [swapped(): lax.ppermute(x, axis, pairs)]
    ppermute x12, waiting for transfers between devices: 10.1 us -> 12.2 us  [swapped(): lax.ppermute(x, axis, pairs)]
  transfers between devices with their start and end apart: 18 -> 18, of which waited for: 10 -> 13; matrix products, arithmetic and copies ran while one was open for 0% -> 0% of each run, Pallas kernels for 11% -> 11%
where the time goes in v5:
time: 117 us; the launch traced here: 116 us
  starting transfers between devices  48.3 us (41%)
  waiting for transfers between devices  33.4 us (29%)
  Pallas kernels  31.6 us (27%)
  between operations  1.38 us (1%)
  local copies, waits for them, and re-layouts  1.35 us (1%)
    all_to_all x6, starting transfers between devices, across(): return lax.all_to_all(slots, axis, split_axis=0, concat_axis=0, tiled=True)  32.8 us
    pallas_call x13, Pallas kernels, run(): kernel(*(x if kind == 's' else pltpu.with_memory_space_constraint(x, pltp...  31.6 us
    all_to_all x6, waiting for transfers between devices, across(): return lax.all_to_all(slots, axis, split_axis=0, concat_axis=0, tiled=True)  21.2 us
    ppermute x12, starting transfers between devices, swapped(): lax.ppermute(x, axis, pairs)  15.5 us
    ppermute x12, waiting for transfers between devices, swapped(): lax.ppermute(x, axis, pairs)  12.2 us
  transfers between devices with their start and end apart: 18, of which 13 were waited for; matrix products, arithmetic and copies ran while one was open for 0% of the time, Pallas kernels for 11%

profile of v5, /device:TPU:1, one launch (start us, length us, event | category | flops | bytes accessed | tf_op | source)
XLA Modules:
  0.0 116.0 jit_solution(16490377400381322889)
XLA Ops:
  1.8 3.2 %collective-permute-start = (f32[8,256]{1,0:T(8,128)S(1)}, f32[8,256]{1,0:T(8,128)S(1)}, u32[]{:S(2)}, u32[]{:S(2)}) collective-permute-start(f32[8,256]{1,0:T(8,128)S(1)} %get-tuple-element.45), channel_id=1, source_target_pairs={{0,1},{1,0},{2,3},{3,2},{4,5},{5,4},{6,7},{7,6},{8,9},{9,8},{10,11... | collective-permute-start | bytes 24584 | tf_op jit(solution)/shard_map/ppermute | solution.py:350
  6.2 4.1 %collective-permute-start.3 = (f32[8,256]{1,0:T(8,128)S(1)}, f32[8,256]{1,0:T(8,128)S(1)}, u32[]{:S(2)}, u32[]{:S(2)}) collective-permute-start(f32[8,256]{1,0:T(8,128)S(1)} %get-tuple-element.48), channel_id=1, source_target_pairs={{16,32},{32,16},{48,64},{64,48},{80,96},{96,80},{112,128},{128,112... | collective-permute-start | bytes 24584 | tf_op jit(solution)/shard_map/ppermute | solution.py:350
  13.1 9.1 %all-to-all-start = ((f32[16,8,128]{2,1,0:T(8,128)}), f32[16,8,128]{2,1,0:T(8,128)S(1)}, u32[]{:S(2)}, u32[]{:S(2)}) async-start(f32[16,8,128]{2,1,0:T(8,128)} %get-tuple-element.53), calls=%async_computation | async-start | bytes 131072 | tf_op jit(solution)/shard_map/all_to_all | solution.py:356
  22.1 2.5 %first_solve.1.present = f32[8,1024]{1,0:T(8,128)S(1)} custom-call(f32[8,1024]{1,0:T(8,128)S(1)} %get-tuple-element.54.scaled, f32[1024,1024]{1,0:T(8,128)} %bitcast.20), custom_call_target="tpu_custom_call" | custom-call | flops 2147483648 | tf_op jit(solution)/shard_map/first_solve/pallas_call | solution.py:36
  24.7 5.3 %all-to-all-done.got = f32[16,8,128]{2,1,0:T(8,128)S(1)} async-done(((f32[16,8,128]{2,1,0:T(8,128)}), f32[16,8,128]{2,1,0:T(8,128)S(1)}, u32[]{:S(2)}, u32[]{:S(2)}) %all-to-all-start) | async-done | bytes 65568 | tf_op jit(solution)/shard_map/all_to_all | solution.py:356
  30.9 5.5 %all-to-all-start.1 = ((f32[16,8,896]{2,1,0:T(8,128)}), f32[16,8,896]{2,1,0:T(8,128)S(1)}, u32[]{:S(2)}, u32[]{:S(2)}) async-start(f32[16,8,896]{2,1,0:T(8,128)} %pack_picked.1), calls=%async_computation.1 | async-start | bytes 917504 | tf_op jit(solution)/shard_map/all_to_all | solution.py:356
  37.0 3.9 %sweep_once.2.present = f32[8,1024]{1,0:T(8,128)S(1)} custom-call(s32[1,1]{1,0:T(1,128)S(6)} %copy.11.elements, f32[8,1024]{1,0:T(8,128)S(1)} %get-tuple-element.54.scaled, f32[8,1024]{1,0:T(8,128)S(1)} %first_solve.1.present, f32[1024,1024]{1,0:T(8,128)} %bitcast.23, f32[1024,1024]{1,0:T(8,128)} %bitcast.21), custom_call_target="tpu_custom_call" | custom-call | flops 4294967296 | tf_op jit(solution)/shard_map/sweep_once/pallas_call | solution.py:36
  40.9 5.2 %all-to-all-done.1.got.asked = f32[16,8,896]{2,1,0:T(8,128)S(1)} async-done(((f32[16,8,896]{2,1,0:T(8,128)}), f32[16,8,896]{2,1,0:T(8,128)S(1)}, u32[]{:S(2)}, u32[]{:S(2)}) %all-to-all-start.1) | async-done | bytes 458784 | tf_op jit(solution)/shard_map/all_to_all | solution.py:356
  46.1 8.7 %coarse_solve.1 = f32[16,8,128]{2,1,0:T(8,128)} custom-call(f32[16,8,896]{2,1,0:T(8,128)S(1)} %all-to-all-done.1.got.asked, f32[48,12288]{1,0:T(8,128)} %coarse.1), custom_call_target="tpu_custom_call" | custom-call | tf_op jit(solution)/shard_map/coarse_solve/pallas_call | solution.py:36
  54.8 5.3 %all-to-all-start.2 = ((f32[16,8,128]{2,1,0:T(8,128)}), f32[16,8,128]{2,1,0:T(8,128)S(1)}, u32[]{:S(2)}, u32[]{:S(2)}) async-start(f32[16,8,128]{2,1,0:T(8,128)} %coarse_solve.1), calls=%async_computation.2 | async-start | bytes 131072 | tf_op jit(solution)/shard_map/all_to_all | solution.py:356
  60.1 3.9 %sweep_once.3.local = f32[8,1024]{1,0:T(8,128)S(1)} custom-call(s32[1,1]{1,0:T(1,128)S(6)} %copy.11.elements, f32[8,1024]{1,0:T(8,128)S(1)} %get-tuple-element.54.scaled, f32[8,1024]{1,0:T(8,128)S(1)} %sweep_once.2.present, f32[1024,1024]{1,0:T(8,128)} %bitcast.24, f32[1024,1024]{1,0:T(8,128)} %bitcast.22), custom_call_target="tpu_custom_call" | custom-call | flops 4294967296 | tf_op jit(solution)/shard_map/sweep_once/pallas_call | solution.py:36
  64.0 3.9 %all-to-all-done.2.got = f32[16,8,128]{2,1,0:T(8,128)S(1)} async-done(((f32[16,8,128]{2,1,0:T(8,128)}), f32[16,8,128]{2,1,0:T(8,128)S(1)}, u32[]{:S(2)}, u32[]{:S(2)}) %all-to-all-start.2) | async-done | bytes 65568 | tf_op jit(solution)/shard_map/all_to_all | solution.py:356
  69.2 3.5 %all-to-all-start.3 = ((f32[16,8,128]{2,1,0:T(8,128)}), f32[16,8,128]{2,1,0:T(8,128)S(1)}, u32[]{:S(2)}, u32[]{:S(2)}) async-start(f32[16,8,128]{2,1,0:T(8,128)} %pack_solved.1), calls=%async_computation.3 | async-start | bytes 131072 | tf_op jit(solution)/shard_map/all_to_all | solution.py:356
  72.7 2.9 %split_matrix.1 = (bf16[1024,1024]{1,0:T(8,128)(2,1)S(1)}, bf16[1024,1024]{1,0:T(8,128)(2,1)S(1)}) custom-call(f32[1024,1024]{1,0:T(8,128)} %bitcast.25), custom_call_target="tpu_custom_call" | custom-call | flops 2147483648 | tf_op jit(solution)/shard_map/split_matrix/pallas_call | solution.py:36
  77.0 2.2 %all-to-all-done.3.got = f32[16,8,128]{2,1,0:T(8,128)S(1)} async-done(((f32[16,8,128]{2,1,0:T(8,128)}), f32[16,8,128]{2,1,0:T(8,128)S(1)}, u32[]{:S(2)}, u32[]{:S(2)}) %all-to-all-start.3) | async-done | bytes 65568 | tf_op jit(solution)/shard_map/all_to_all | solution.py:356
  81.9 1.9 %collective-permute-start.7 = (f32[8,256]{1,0:T(8,128)S(1)}, f32[8,256]{1,0:T(8,128)S(1)}, u32[]{:S(2)}, u32[]{:S(2)}) collective-permute-start(f32[8,256]{1,0:T(8,128)S(1)} %get-tuple-element.70), channel_id=1, source_target_pairs={{16,32},{32,16},{48,64},{64,48},{80,96},{96,80},{112,128},{128,112... | collective-permute-start | bytes 24584 | tf_op jit(solution)/shard_map/ppermute | solution.py:350
  84.2 3.5 %collective-permute-done.7.g3 = f32[8,256]{1,0:T(8,128)S(1)} collective-permute-done((f32[8,256]{1,0:T(8,128)S(1)}, f32[8,256]{1,0:T(8,128)S(1)}, u32[]{:S(2)}, u32[]{:S(2)}) %collective-permute-start.7) | collective-permute-done | bytes 8224 | tf_op jit(solution)/shard_map/ppermute | solution.py:350
  87.7 3.2 %apply_operator.1 = (f32[8,1024]{1,0:T(8,128)S(1)}, f32[8,1024]{1,0:T(8,128)S(1)}, f32[8,256]{1,0:T(8,128)S(1)}, f32[8,256]{1,0:T(8,128)S(1)}, f32[8,256]{1,0:T(...) custom-call(f32[8,1024]{1,0:T(8,128)S(1)} %get-tuple-element.66.t, f32[8,256]{1,0:T(8,128)S(1)} %collective-permute-done.4.g0, ...), custom_call_target="tpu_custom_call" | custom-call | tf_op jit(solution)/shard_map/apply_operator/pallas_call | solution.py:36
  90.9 5.9 %all-to-all-start.4 = ((f32[16,8,128]{2,1,0:T(8,128)}), f32[16,8,128]{2,1,0:T(8,128)S(1)}, u32[]{:S(2)}, u32[]{:S(2)}) async-start(f32[16,8,128]{2,1,0:T(8,128)} %get-tuple-element.74), calls=%async_computation.4 | async-start | bytes 131072 | tf_op jit(solution)/shard_map/all_to_all | solution.py:356
  96.8 1.9 %collective-permute-start.9 = (f32[8,256]{1,0:T(8,128)S(1)}, f32[8,256]{1,0:T(8,128)S(1)}, u32[]{:S(2)}, u32[]{:S(2)}) collective-permute-start(f32[8,256]{1,0:T(8,128)S(1)} %get-tuple-element.76), channel_id=1, source_target_pairs={{16,32},{32,16},{48,64},{64,48},{80,96},{96,80},{112,128},{128,112... | collective-permute-start | bytes 24584 | tf_op jit(solution)/shard_map/ppermute | solution.py:350
  99.3 3.5 %collective-permute-done.9.g3 = f32[8,256]{1,0:T(8,128)S(1)} collective-permute-done((f32[8,256]{1,0:T(8,128)S(1)}, f32[8,256]{1,0:T(8,128)S(1)}, u32[]{:S(2)}, u32[]{:S(2)}) %collective-permute-start.9) | collective-permute-done | bytes 8224 | tf_op jit(solution)/shard_map/ppermute | solution.py:350
  105.2 3.5 %all-to-all-start.5 = ((f32[16,8,128]{2,1,0:T(8,128)}), f32[16,8,128]{2,1,0:T(8,128)S(1)}, u32[]{:S(2)}, u32[]{:S(2)}) async-start(f32[16,8,128]{2,1,0:T(8,128)} %subtotal.1), calls=%async_computation.5 | async-start | bytes 131072 | tf_op jit(solution)/shard_map/all_to_all | solution.py:356
  109.9 2.3 %collective-permute-done.11.g1 = f32[8,256]{1,0:T(8,128)S(1)} collective-permute-done((f32[8,256]{1,0:T(8,128)S(1)}, f32[8,256]{1,0:T(8,128)S(1)}, u32[]{:S(2)}, u32[]{:S(2)}) %collective-permute-start.11) | collective-permute-done | bytes 8224 | tf_op jit(solution)/shard_map/ppermute | solution.py:350
  112.2 2.9 %all-to-all-done.5.got = f32[16,8,128]{2,1,0:T(8,128)S(1)} async-done(((f32[16,8,128]{2,1,0:T(8,128)}), f32[16,8,128]{2,1,0:T(8,128)S(1)}, u32[]{:S(2)}, u32[]{:S(2)}) %all-to-all-start.5) | async-done | bytes 65568 | tf_op jit(solution)/shard_map/all_to_all | solution.py:356
  (27 shorter events, 16.8 us)
Async XLA Ops:
  1.8 8.5 %collective-permute-start = (f32[8,256]{1,0:T(8,128)S(1)}, f32[8,256]{1,0:T(8,128)S(1)}, u32[]{:S(2)}, u32[]{:S(2)}) collective-permute-start(f32[8,256]{1,0:T(8,128)S(1)} %get-tuple-element.45), channel_id=1, source_target_pairs={{0,1},{1,0},{2,3},{3,2},{4,5},{5,4},{6,7},{7,6},{8,9},{9,8},{10,11... | collective-permute-start | bytes 24584 | tf_op jit(solution)/shard_map/ppermute | solution.py:350
  5.0 5.3 %collective-permute-start.1 = (f32[8,256]{1,0:T(8,128)S(1)}, f32[8,256]{1,0:T(8,128)S(1)}, u32[]{:S(2)}, u32[]{:S(2)}) collective-permute-start(f32[8,256]{1,0:T(8,128)S(1)} %get-tuple-element.46), channel_id=1, source_target_pairs={{1,2},{2,1},{3,4},{4,3},{5,6},{6,5},{7,8},{8,7},{9,10},{10,9},{11,... | collective-permute-start | bytes 24584 | tf_op jit(solution)/shard_map/ppermute | solution.py:350
  5.0 5.3 %collective-permute-start.2 = (f32[8,256]{1,0:T(8,128)S(1)}, f32[8,256]{1,0:T(8,128)S(1)}, u32[]{:S(2)}, u32[]{:S(2)}) collective-permute-start(f32[8,256]{1,0:T(8,128)S(1)} %get-tuple-element.47), channel_id=1, source_target_pairs={{0,16},{16,0},{32,48},{48,32},{64,80},{80,64},{96,112},{112,96},{1... | collective-permute-start | bytes 24584 | tf_op jit(solution)/shard_map/ppermute | solution.py:350
  6.2 5.8 %collective-permute-start.3 = (f32[8,256]{1,0:T(8,128)S(1)}, f32[8,256]{1,0:T(8,128)S(1)}, u32[]{:S(2)}, u32[]{:S(2)}) collective-permute-start(f32[8,256]{1,0:T(8,128)S(1)} %get-tuple-element.48), channel_id=1, source_target_pairs={{16,32},{32,16},{48,64},{64,48},{80,96},{96,80},{112,128},{128,112... | collective-permute-start | bytes 24584 | tf_op jit(solution)/shard_map/ppermute | solution.py:350
  13.1 16.9 %all-to-all-start = ((f32[16,8,128]{2,1,0:T(8,128)}), f32[16,8,128]{2,1,0:T(8,128)S(1)}, u32[]{:S(2)}, u32[]{:S(2)}) async-start(f32[16,8,128]{2,1,0:T(8,128)} %get-tuple-element.53), calls=%async_computation | async-start | bytes 131072 | tf_op jit(solution)/shard_map/all_to_all | solution.py:356
  30.9 15.2 %all-to-all-start.1 = ((f32[16,8,896]{2,1,0:T(8,128)}), f32[16,8,896]{2,1,0:T(8,128)S(1)}, u32[]{:S(2)}, u32[]{:S(2)}) async-start(f32[16,8,896]{2,1,0:T(8,128)} %pack_picked.1), calls=%async_computation.1 | async-start | bytes 917504 | tf_op jit(solution)/shard_map/all_to_all | solution.py:356
  54.8 13.1 %all-to-all-start.2 = ((f32[16,8,128]{2,1,0:T(8,128)}), f32[16,8,128]{2,1,0:T(8,128)S(1)}, u32[]{:S(2)}, u32[]{:S(2)}) async-start(f32[16,8,128]{2,1,0:T(8,128)} %coarse_solve.1), calls=%async_computation.2 | async-start | bytes 131072 | tf_op jit(solution)/shard_map/all_to_all | solution.py:356
  69.2 10.0 %all-to-all-start.3 = ((f32[16,8,128]{2,1,0:T(8,128)}), f32[16,8,128]{2,1,0:T(8,128)S(1)}, u32[]{:S(2)}, u32[]{:S(2)}) async-start(f32[16,8,128]{2,1,0:T(8,128)} %pack_solved.1), calls=%async_computation.3 | async-start | bytes 131072 | tf_op jit(solution)/shard_map/all_to_all | solution.py:356
  75.6 1.4 %copy-start = (bf16[1024,1024]{1,0:T(8,128)(2,1)}, bf16[1024,1024]{1,0:T(8,128)(2,1)S(1)}, u32[]{:S(2)}) copy-start(bf16[1024,1024]{1,0:T(8,128)(2,1)S(1)} %get-tuple-element.72.low) | copy-start | bytes 6291460
  79.8 4.0 %collective-permute-start.4 = (f32[8,256]{1,0:T(8,128)S(1)}, f32[8,256]{1,0:T(8,128)S(1)}, u32[]{:S(2)}, u32[]{:S(2)}) collective-permute-start(f32[8,256]{1,0:T(8,128)S(1)} %get-tuple-element.67), channel_id=1, source_target_pairs={{0,1},{1,0},{2,3},{3,2},{4,5},{5,4},{6,7},{7,6},{8,9},{9,8},{10,11... | collective-permute-start | bytes 24584 | tf_op jit(solution)/shard_map/ppermute | solution.py:350
  81.1 3.1 %collective-permute-start.5 = (f32[8,256]{1,0:T(8,128)S(1)}, f32[8,256]{1,0:T(8,128)S(1)}, u32[]{:S(2)}, u32[]{:S(2)}) collective-permute-start(f32[8,256]{1,0:T(8,128)S(1)} %get-tuple-element.68), channel_id=1, source_target_pairs={{1,2},{2,1},{3,4},{4,3},{5,6},{6,5},{7,8},{8,7},{9,10},{10,9},{11,... | collective-permute-start | bytes 24584 | tf_op jit(solution)/shard_map/ppermute | solution.py:350
  81.6 2.6 %collective-permute-start.6 = (f32[8,256]{1,0:T(8,128)S(1)}, f32[8,256]{1,0:T(8,128)S(1)}, u32[]{:S(2)}, u32[]{:S(2)}) collective-permute-start(f32[8,256]{1,0:T(8,128)S(1)} %get-tuple-element.69), channel_id=1, source_target_pairs={{0,16},{16,0},{32,48},{48,32},{64,80},{80,64},{96,112},{112,96},{1... | collective-permute-start | bytes 24584 | tf_op jit(solution)/shard_map/ppermute | solution.py:350
  81.9 5.8 %collective-permute-start.7 = (f32[8,256]{1,0:T(8,128)S(1)}, f32[8,256]{1,0:T(8,128)S(1)}, u32[]{:S(2)}, u32[]{:S(2)}) collective-permute-start(f32[8,256]{1,0:T(8,128)S(1)} %get-tuple-element.70), channel_id=1, source_target_pairs={{16,32},{32,16},{48,64},{64,48},{80,96},{96,80},{112,128},{128,112... | collective-permute-start | bytes 24584 | tf_op jit(solution)/shard_map/ppermute | solution.py:350
  90.9 13.7 %all-to-all-start.4 = ((f32[16,8,128]{2,1,0:T(8,128)}), f32[16,8,128]{2,1,0:T(8,128)S(1)}, u32[]{:S(2)}, u32[]{:S(2)}) async-start(f32[16,8,128]{2,1,0:T(8,128)} %get-tuple-element.74), calls=%async_computation.4 | async-start | bytes 131072 | tf_op jit(solution)/shard_map/all_to_all | solution.py:356
  96.8 2.5 %collective-permute-start.8 = (f32[8,256]{1,0:T(8,128)S(1)}, f32[8,256]{1,0:T(8,128)S(1)}, u32[]{:S(2)}, u32[]{:S(2)}) collective-permute-start(f32[8,256]{1,0:T(8,128)S(1)} %get-tuple-element.75), channel_id=1, source_target_pairs={{0,16},{16,0},{32,48},{48,32},{64,80},{80,64},{96,112},{112,96},{1... | collective-permute-start | bytes 24584 | tf_op jit(solution)/shard_map/ppermute | solution.py:350
  96.8 6.0 %collective-permute-start.9 = (f32[8,256]{1,0:T(8,128)S(1)}, f32[8,256]{1,0:T(8,128)S(1)}, u32[]{:S(2)}, u32[]{:S(2)}) collective-permute-start(f32[8,256]{1,0:T(8,128)S(1)} %get-tuple-element.76), channel_id=1, source_target_pairs={{16,32},{32,16},{48,64},{64,48},{80,96},{96,80},{112,128},{128,112... | collective-permute-start | bytes 24584 | tf_op jit(solution)/shard_map/ppermute | solution.py:350
  105.2 9.9 %all-to-all-start.5 = ((f32[16,8,128]{2,1,0:T(8,128)}), f32[16,8,128]{2,1,0:T(8,128)S(1)}, u32[]{:S(2)}, u32[]{:S(2)}) async-start(f32[16,8,128]{2,1,0:T(8,128)} %subtotal.1), calls=%async_computation.5 | async-start | bytes 131072 | tf_op jit(solution)/shard_map/all_to_all | solution.py:356
  108.7 1.3 %collective-permute-start.10 = (f32[8,256]{1,0:T(8,128)S(1)}, f32[8,256]{1,0:T(8,128)S(1)}, u32[]{:S(2)}, u32[]{:S(2)}) collective-permute-start(f32[8,256]{1,0:T(8,128)S(1)} %get-tuple-element.78), channel_id=1, source_target_pairs={{0,1},{1,0},{2,3},{3,2},{4,5},{5,4},{6,7},{7,6},{8,9},{9,8},{10,11... | collective-permute-start | bytes 24584 | tf_op jit(solution)/shard_map/ppermute | solution.py:350
  108.9 3.3 %collective-permute-start.11 = (f32[8,256]{1,0:T(8,128)S(1)}, f32[8,256]{1,0:T(8,128)S(1)}, u32[]{:S(2)}, u32[]{:S(2)}) collective-permute-start(f32[8,256]{1,0:T(8,128)S(1)} %get-tuple-element.79), channel_id=1, source_target_pairs={{1,2},{2,1},{3,4},{4,3},{5,6},{6,5},{7,8},{8,7},{9,10},{10,9},{11,... | collective-permute-start | bytes 24584 | tf_op jit(solution)/shard_map/ppermute | solution.py:350
